TPU v7x, 32 devices: a whole 2x2x4 slice. The times are simulated.
32 devices in a mesh: depth: 8 (over z, x), col: 4 (over y, core).
Axes of the slice: x: 2, y: 2, z: 4, core: 2. Of those that a mesh axis runs over, the one named last changes fastest.
Arguments:
- recorded: bfloat16 [4, 16, 2, 512, 512], P(None, 'depth', None, 'col'), may hold values from -6 to 6
- vertical: float32 [4, 512], replicated, may hold values from 0.05 to 0.8
Outputs:
- prediction: float32 [4, 2, 512, 512], P(None, None, 'col', 'depth')
All inputs are finite; a program needn't handle non-finite values.
Results may differ from a plain program's by a relative error of at most 0.01.
Values may be sent and summed in bfloat16 or wider, within the bound.
A program may use at most 64 MiB of HBM per device.

v0:
```python
import functools

import jax
import jax.numpy as jnp
from jax import lax
from jax.experimental import pallas as pl
from jax.experimental.pallas import tpu as pltpu
from jax.sharding import PartitionSpec as P

MESH = pl.DeviceIdType.MESH
SPLITS = 4


def prefix(x, axis, combine, identity):
    peers, mine = (lax.axis_size(axis), lax.axis_index(axis))
    everything = lax.all_gather(x, axis)
    start = jnp.broadcast_to(jnp.asarray(identity, x.dtype), x.shape)

    def lap(k, before):
        at = peers - 1 - k
        reached = at > mine
        new = combine(before, everything[at])
        return jnp.where(reached, new, before)

    return lax.fori_loop(0, peers, lap, start)


def from_behind(value, axis, steps):
    count = lax.axis_size(axis)
    initial, last = (max(0, -steps), min(count, count - steps))
    return lax.ppermute(value, axis, [(source, source + steps) for source in range(initial, last)])


def complex_product(left_side, right_side, pattern, stack_axis):
    left_real = left_side[:, :, 0]
    left_imag = left_side[:, :, 1]
    right_real = right_side[:, :, 0]
    right_imag = right_side[:, :, 1]
    real_part = jnp.einsum(
        pattern, left_real, right_real, preferred_element_type=jnp.float32
    ) - jnp.einsum(pattern, left_imag, right_imag, preferred_element_type=jnp.float32)
    imag_part = jnp.einsum(
        pattern, left_real, right_imag, preferred_element_type=jnp.float32
    ) + jnp.einsum(pattern, left_imag, right_real, preferred_element_type=jnp.float32)
    return jnp.stack([real_part, imag_part], axis=stack_axis)


def add_pair(earlier, later):
    return earlier + later


def shards(recorded, vertical):
    local_depths = recorded.shape[1]
    row_count = recorded.shape[3]
    depth_cells = lax.axis_size("depth") * local_depths
    depth_step = 1.0 / depth_cells
    first_row = lax.axis_index("col") * row_count
    row_wave = lax.dynamic_slice_in_dim(vertical, first_row, row_count, 1)
    depth_f = (
        lax.axis_index("depth") * local_depths + jnp.arange(local_depths, dtype=jnp.int32)
    ).astype(jnp.float32)
    phase_angle = (row_wave[:, None, :, None] + vertical[:, None, None, :]) * depth_f[
        None, :, None, None
    ]
    cosine = jnp.cos(phase_angle)
    sine_part = jnp.sin(phase_angle)
    real_in = recorded[:, :, 0].astype(jnp.float32)
    imag_in = recorded[:, :, 1].astype(jnp.float32)
    plus32 = (
        jnp.stack(
            [real_in * cosine - imag_in * sine_part, real_in * sine_part + imag_in * cosine], axis=2
        )
        * depth_step
    )
    minus_phase = (
        jnp.stack(
            [real_in * cosine + imag_in * sine_part, imag_in * cosine - real_in * sine_part], axis=2
        )
        * depth_step
    ).astype(jnp.bfloat16)
    inner_sum = lax.cumsum(plus32, axis=1, reverse=True)
    beyond = prefix(inner_sum[:, 0], "depth", add_pair, jnp.zeros_like(inner_sum[:, 0]))
    suffix_all = inner_sum + beyond[:, None]
    following = from_behind(suffix_all[:, 0], "depth", -1)
    tail_sum = jnp.concatenate([suffix_all[:, 1:], following[:, None]], axis=1).astype(jnp.bfloat16)
    columns = tail_sum
    middle = complex_product(
        columns, lax.all_gather(minus_phase, "col", axis=3, tiled=True), "wzrk,wzkc->wzrc", 2
    ).astype(jnp.bfloat16)
    columns = middle
    partial_pred = complex_product(
        columns, lax.all_gather(tail_sum, "col", axis=3, tiled=True), "wzrk,wzkc->wrc", 1
    )
    return lax.psum_scatter(partial_pred, "depth", scatter_dimension=3, tiled=True)


def kernel(
    sizes, rec, vertical, out, waves, table, ct, rt, land, ml, tl, ts, prod, suf, sbuf, srecv, ein, eout, xsend, xrecv,
    pacc, psend, precv, qsend, qrecv, qsum, fsend, frecv,
    v_sem, a_send, a_recv, s_send, s_recv, e_send, e_recv, x_send, x_recv, p_send, p_recv,
    q_send, q_recv, f_send, f_recv,
):
    levels, freqs, cols, local, rows, size, width, splits = sizes
    depth, col = lax.axis_index("depth"), lax.axis_index("col")
    z, x = depth // 2, depth % 2
    y, core = col // 2, col % 2
    rings = cols // 2
    chunks = size // width
    sub = rows // splits
    share_rows = cols * sub // 2
    me = y * 2 + x
    f32, bf16 = jnp.float32, jnp.bfloat16

    def device(zz, xx, yy, cc):
        return (zz * 2 + xx, yy * 2 + cc)

    other_core = device(z, x, y, 1 - core)
    fetch = pltpu.make_async_copy(vertical, waves, v_sem)
    fetch.start()
    barrier = pltpu.get_barrier_semaphore()
    greeted = 0
    for dx in range(2):
        for dc in range(cols):
            if dx or dc:
                pl.semaphore_signal(
                    barrier, inc=1,
                    device_id=(z * 2 + (x + dx) % 2, (col + dc) % cols), device_id_type=MESH,
                )
                greeted += 1
    for dz in range(1, levels):
        pl.semaphore_signal(
            barrier, inc=1, device_id=(((z + dz) % levels) * 2 + x, col), device_id_type=MESH
        )
        greeted += 1
    pl.semaphore_wait(barrier, greeted)

    def remote(src, dst, send, recv, to):
        return pltpu.make_async_remote_copy(
            src_ref=src, dst_ref=dst, send_sem=send, recv_sem=recv, device_id=to, device_id_type=MESH
        )

    pieces = [(j, r) for j in range(chunks) for r in range(splits)]

    def spread(n, dx, dy, near=False):
        j, r = pieces[n]
        xx, yy = (x + dx) % 2, (y + dy) % rings
        w = yy * 2 + xx
        lanes = pl.ds(j * width, width)
        src = rec.at[w, :, :, pl.ds(r * sub, sub), lanes]
        dst = land.at[:, :, pl.ds(pl.multiple_of(col * rows + r * sub, sub), sub), lanes]
        if near:
            return pltpu.make_async_copy(src, dst, a_recv.at[n, col])
        return remote(src, dst, a_send.at[n, dy * 2 + dx], a_recv.at[n, col], device(z, xx, yy, x))

    routes = [(dx, dy) for dy in reversed(range(rings)) for dx in (1, 0)]
    for n in range(len(pieces)):
        for dx, dy in routes:
            if dx or dy:
                spread(n, dx, dy).start()
            else:
                pl.when(core == x)(lambda: spread(n, dx, dy, near=True).start())
                pl.when(core != x)(lambda: spread(n, dx, dy).start())

    @pl.when(z == levels - 1)
    def _():
        ein[...] = jnp.zeros_like(ein)

    fetch.wait()
    wave = waves[pl.ds(me, 1), :]
    table[...] = jnp.zeros_like(table)
    for l in range(local):
        angle = wave * ((z * 2 + core) * local + l).astype(f32)
        table[2 * l : 2 * l + 1, :] = jnp.cos(angle)
        table[2 * l + 1 : 2 * l + 2, :] = jnp.sin(angle)
    ct[...] = table[...].T
    rt[...] = table[0 : 2 * local, :] * (1.0 / (2 * levels * local))

    tile = sub

    def phase(n):
        j, r = pieces[n]
        for source in range(cols):
            dst = land.at[:, :, pl.ds(source * rows + r * sub, sub), pl.ds(j * width, width)]
            pltpu.make_async_copy(dst, dst, a_recv.at[n, source]).wait()
        lanes = pl.ds(j * width, width)

        @pl.loop(0, cols)
        def _(t):
            start = pl.multiple_of(t * rows + r * sub, sub)
            at = pl.ds(start, tile)
            low = pl.ds(start + size, tile)
            sum_re = sum_im = None
            for l in reversed(range(local)):
                if sum_re is not None:
                    suf[l, 0, at, lanes] = sum_re
                    suf[l, 1, at, lanes] = sum_im
                re = land[l, 0, at, lanes].astype(f32)
                im = land[l, 1, at, lanes].astype(f32)
                row_cos, row_sin = ct[at, 2 * l : 2 * l + 1], ct[at, 2 * l + 1 : 2 * l + 2]
                col_cos, col_sin = rt[2 * l : 2 * l + 1, lanes], rt[2 * l + 1 : 2 * l + 2, lanes]
                cosine = row_cos * col_cos - row_sin * col_sin
                sine = row_sin * col_cos + row_cos * col_sin
                a, b, c, d = re * cosine, im * sine, re * sine, im * cosine
                minus_re, minus_im = a + b, d - c
                shifted = pl.ds(size + j * width, width)
                ml[l, at, lanes] = minus_re.astype(bf16)
                ml[l, low, shifted] = minus_re.astype(bf16)
                ml[l, at, shifted] = (-minus_im).astype(bf16)
                ml[l, low, lanes] = minus_im.astype(bf16)
                plus_re, plus_im = a - b, c + d
                sum_re = plus_re if sum_re is None else sum_re + plus_re
                sum_im = plus_im if sum_im is None else sum_im + plus_im
            packed = pl.ds(pl.multiple_of(t * sub, sub), sub)
            sbuf[n, 0, packed, :] = sum_re.astype(bf16)
            sbuf[n, 1, packed, :] = sum_im.astype(bf16)

        share(n).start()

    def share(j):
        theirs = pl.ds(pl.multiple_of((1 - core) * share_rows, share_rows), share_rows)
        return remote(sbuf.at[j, :, theirs, :], srecv.at[j], s_send.at[j], s_recv.at[j], other_core)

    def down(j):
        to = device((z + levels - 1) % levels, x, y, core)
        return remote(eout.at[j], ein.at[j], e_send.at[j], e_recv.at[j], to)

    def across(j):
        return remote(xsend.at[j], xrecv.at[j], x_send.at[j], x_recv.at[j], other_core)

    def put_tail(n, start, deeper):
        j = pieces[n][0]
        at, low = pl.ds(start, tile), pl.ds(start + size, tile)
        lanes = pl.ds(j * width, width)
        for l in range(local):
            re, im = deeper
            if l < local - 1:
                re, im = re + suf[l, 0, at, lanes], im + suf[l, 1, at, lanes]
            base = 2 * size * l
            first = pl.ds(base + j * width, width)
            second = pl.ds(base + size + j * width, width)
            ts[l, at, lanes] = re.astype(bf16)
            ts[l, low, lanes] = im.astype(bf16)
            tl[at, first] = re.astype(bf16)
            tl[low, second] = re.astype(bf16)
            tl[at, second] = (-im).astype(bf16)
            tl[low, first] = im.astype(bf16)

    def chain(n):
        r = pieces[n][1]
        share(n).wait_recv()
        pl.when(z < levels - 1)(lambda: down(n).wait_recv())

        @pl.loop(0, cols // 2)
        def _(t):
            start = pl.multiple_of(t * sub, sub)
            at = pl.ds(start, sub)
            mine = pl.ds(pl.multiple_of(core * share_rows + start, sub), sub)
            for part in range(2):
                below = ein[n, part, at, :].astype(f32)
                own = sbuf[n, part, mine, :].astype(f32)
                their = srecv[n, part, at, :].astype(f32)
                eout[n, part, at, :] = (below + own + their).astype(bf16)
                xsend[n, part, at, :] = (below + jnp.where(core == 1, own, 0.0)).astype(bf16)

        pl.when(z > 0)(lambda: down(n).start())
        across(n).start()

        @pl.loop(0, cols // 2)
        def _(t):
            at = pl.ds(pl.multiple_of(t * sub, sub), sub)
            deeper = [
                ein[n, part, at, :].astype(f32)
                + jnp.where(core == 0, srecv[n, part, at, :].astype(f32), 0.0)
                for part in range(2)
            ]
            start = (core * (cols // 2) + t) * rows + r * sub
            put_tail(n, pl.multiple_of(start, sub), deeper)

    def finish(n):
        r = pieces[n][1]
        across(n).wait_recv()

        @pl.loop(0, cols // 2)
        def _(t):
            at = pl.ds(pl.multiple_of(t * sub, sub), sub)
            deeper = [xrecv[n, part, at, :].astype(f32) for part in range(2)]
            start = ((1 - core) * (cols // 2) + t) * rows + r * sub
            put_tail(n, pl.multiple_of(start, sub), deeper)

    block = 2 * width
    blocks = size // block

    def middle(h):
        lanes = pl.ds(h * block, block)
        for l in range(local):
            @pl.loop(0, 2 * cols // 2)
            def _(t):
                at = pl.ds(pl.multiple_of(t * 2 * rows, 2 * rows), 2 * rows)
                low = pl.ds(pl.multiple_of(2 * size * l + t * 2 * rows, 2 * rows), 2 * rows)
                prod[low, lanes] = jnp.dot(
                    ml[l, at, :], ts[l, :, lanes], preferred_element_type=f32
                ).astype(bf16)

    last = len(pieces) - 1

    def early():
        for h in range(blocks - 1):
            middle(h)

    for n in range(last):
        phase(n)
        chain(n)
        if n > 0:
            finish(n - 1)
    phase(last)
    finish(last - 1)
    pl.when(z < levels - 1)(early)
    chain(last)
    pl.when(z == levels - 1)(early)
    finish(last)
    middle(blocks - 1)

    tiles = 2 * rings
    order = [(z // 2 + 1 + i) % blocks for i in range(blocks)]

    def pair(i):
        return remote(psend.at[i], precv.at[i], p_send.at[i], p_recv.at[i], other_core)

    for i, h in enumerate(order):
        lanes = pl.ds(pl.multiple_of(h * block, block), block)

        @pl.loop(0, tiles)
        def _(t):
            at = pl.ds(pl.multiple_of(t * 2 * rows, 2 * rows), 2 * rows)
            pacc[i, t] = jnp.dot(tl[at, :], prod[:, lanes], preferred_element_type=f32)
            theirs = pl.ds(pl.multiple_of((1 - core) * rows, rows), rows)
            psend[i, t] = pacc[i, t, theirs, :].astype(bf16)

        pair(i).start()

    def to_level(target):
        return remote(
            qsend.at[target], qrecv.at[z], q_send.at[target], q_recv.at[z],
            device(target, x, y, core),
        )

    for i, h in enumerate(order):
        pair(i).wait_recv()
        for s in range(2):
            target = h * 2 + s
            lanes = pl.ds(s * width, width)

            @pl.loop(0, tiles)
            def _(t):
                mine = pl.ds(pl.multiple_of(core * rows, rows), rows)
                q = pacc[i, t, mine, lanes] + precv[i, t, :, lanes].astype(f32)
                qsend[target, t] = q.astype(bf16)

                @pl.when(target == z)
                def _():
                    qsum[t] = q

            pl.when(target != z)(lambda: to_level(target).start())

    for dz in range(1, levels):
        source = (z + dz) % levels
        remote(
            qsend.at[source], qrecv.at[source], q_send.at[source], q_recv.at[source],
            device(source, x, y, core),
        ).wait_recv()

        @pl.loop(0, tiles)
        def _(t):
            qsum[t] += qrecv[source, t].astype(f32)

    narrow = width // 2

    def joined(yy, xx):
        lanes = slice(xx * narrow, (xx + 1) * narrow)
        return jnp.concatenate([qsum[yy][:, lanes], qsum[rings + yy][:, lanes]], axis=1)

    for yy in range(rings):
        for xx in range(2):
            fsend[yy, xx] = joined(yy, xx).astype(bf16)

    def to_rows(dx, dy):
        xx, yy = (x + dx) % 2, (y + dy) % rings
        return remote(
            fsend.at[yy, xx], frecv.at[me], f_send.at[dy * 2 + dx], f_recv.at[me],
            device(z, xx, yy, core),
        )

    for dx, dy in routes:
        if dx or dy:
            to_rows(dx, dy).start()
    out[me] = jnp.where(x == 0, joined(y, 0), joined(y, 1))
    for dx, dy in reversed(routes):
        if dx or dy:
            xx, yy = (x + dx) % 2, (y + dy) % rings
            w = yy * 2 + xx
            remote(
                fsend.at[yy, xx], frecv.at[w], f_send.at[dy * 2 + dx], f_recv.at[w],
                device(z, xx, yy, core),
            ).wait_recv()
            out[w] = frecv[w].astype(f32)

    for n in range(len(pieces)):
        for dx, dy in routes:
            if dx or dy:
                spread(n, dx, dy).wait_send()
            else:
                pl.when(core != x)(lambda: spread(n, dx, dy).wait_send())
        share(n).wait_send()
        pl.when(z > 0)(lambda: down(n).wait_send())
        across(n).wait_send()
    for i in range(blocks):
        pair(i).wait_send()
    for dz in range(1, levels):
        to_level((z + dz) % levels).wait_send()
    for dx, dy in routes:
        if dx or dy:
            to_rows(dx, dy).wait_send()


def fused(recorded, vertical):
    freqs, local, _, rows, size = recorded.shape
    depths, cols = lax.axis_size("depth"), lax.axis_size("col")
    levels, chunks_wide = depths // 2, 2 * size // depths
    width = chunks_wide
    chunks, tiles, blocks = size // width, cols, size // (2 * width)
    pieces, share_rows = chunks * SPLITS, rows * cols // SPLITS // 2
    sizes = (levels, freqs, cols, local, rows, size, width, SPLITS)
    f32, bf16 = jnp.float32, jnp.bfloat16
    dma = pltpu.SemaphoreType.DMA
    packed = pl.pallas_call(
        functools.partial(kernel, sizes),
        out_shape=jax.ShapeDtypeStruct((freqs, rows, width), f32),
        in_specs=[
            pl.BlockSpec(memory_space=pl.ANY),
            pl.BlockSpec(memory_space=pl.ANY),
        ],
        out_specs=pl.BlockSpec(memory_space=pltpu.VMEM),
        scratch_shapes=[
            pltpu.VMEM((freqs, size), f32),
            pltpu.VMEM((128, size), f32),
            pltpu.VMEM((size, 128), f32),
            pltpu.VMEM((2 * local, size), f32),
            pltpu.VMEM((local, 2, size, size), bf16),
            pltpu.VMEM((local, 2 * size, 2 * size), bf16),
            pltpu.VMEM((2 * size, local * 2 * size), bf16),
            pltpu.VMEM((local, 2 * size, size), bf16),
            pltpu.VMEM((local * 2 * size, size), bf16),
            pltpu.VMEM((local - 1, 2, size, size), f32),
            pltpu.VMEM((pieces, 2, 2 * share_rows, width), bf16),
            pltpu.VMEM((pieces, 2, share_rows, width), bf16),
            pltpu.VMEM((pieces, 2, share_rows, width), bf16),
            pltpu.VMEM((pieces, 2, share_rows, width), bf16),
            pltpu.VMEM((pieces, 2, share_rows, width), bf16),
            pltpu.VMEM((pieces, 2, share_rows, width), bf16),
            pltpu.VMEM((blocks, tiles, 2 * rows, 2 * width), f32),
            pltpu.VMEM((blocks, tiles, rows, 2 * width), bf16),
            pltpu.VMEM((blocks, tiles, rows, 2 * width), bf16),
            pltpu.VMEM((levels, tiles, rows, width), bf16),
            pltpu.VMEM((levels, tiles, rows, width), bf16),
            pltpu.VMEM((tiles, rows, width), f32),
            pltpu.VMEM((cols // 2, 2, rows, width), bf16),
            pltpu.VMEM((freqs, rows, width), bf16),
            dma, dma((pieces, cols)), dma((pieces, cols)),
            dma((pieces,)), dma((pieces,)),
            dma((pieces,)), dma((pieces,)),
            dma((pieces,)), dma((pieces,)),
            dma((blocks,)), dma((blocks,)),
            dma((levels,)), dma((levels,)),
            dma((cols,)), dma((freqs,)),
        ],
        compiler_params=pltpu.CompilerParams(
            collective_id=0, has_side_effects=True, vmem_limit_bytes=56 * 1024 * 1024
        ),
        name="prediction",
    )(recorded, vertical)
    return packed.reshape(freqs, rows, 2, width // 2).transpose(0, 2, 1, 3)


def body(recorded, vertical):
    freqs, local, _, rows, size = recorded.shape
    depths, cols = lax.axis_size("depth"), lax.axis_size("col")
    fits = cols == freqs and cols % 2 == 0 and depths % 4 == 0 and local > 1
    fits = fits and rows % 128 == 0 and (2 * size // depths) % 128 == 0
    return fused(recorded, vertical) if fits else shards(recorded, vertical)


def solution(mesh):
    in_specs = (P(None, "depth", None, "col", None), P())
    out_specs = P(None, None, "col", "depth")
    return jax.shard_map(body, mesh=mesh, in_specs=in_specs, out_specs=out_specs, check_vma=False)
```

profile of v0, /device:TPU:8, one launch (start us, length us, event | category | flops | bytes accessed | tf_op | source)
XLA Modules:
  0.0 68.1 jit_solution(12812215138300802949)
XLA Ops:
  0.0 66.3 %prediction.1 = f32[4,128,128]{2,1,0:T(8,128)} custom-call(bf16[4,2,2,128,512]{4,3,2,1,0:T(8,128)(2,1)} %rec.1, f32[4,512]{1,0:T(4,128)} %vertical.1), custom_call_target="tpu_custom_call" | custom-call | tf_op jit(solution)/shard_map/prediction/pallas_call | solution.py:435
  66.3 1.8 %copy.4 = f32[4,128,128]{1,2,0:T(8,128)} copy(f32[4,128,128]{2,1,0:T(8,128)} %prediction.1) | data formatting | bytes 524288 | tf_op jit(solution)/shard_map/prediction/pallas_call | solution.py:435
where the time goes:
time: 68.3 us; the launch traced here: 68.1 us
  Pallas kernels  66.3 us (97%)
  local copies, waits for them, and re-layouts  1.79 us (3%)
    pallas_call x1, Pallas kernels, fused(): pl.pallas_call(functools.partial(kernel, sizes), out_shape=jax.ShapeDtype...  66.3 us
    pallas_call x1, local copies, waits for them, and re-layouts, fused(): pl.pallas_call(functools.partial(kernel, sizes), out_shape=jax.ShapeDtype...  1.79 us

commit v1 on v0

v1 whole, which is shorter than its diff:
```python
import functools

import jax
import jax.numpy as jnp
from jax import lax
from jax.experimental import pallas as pl
from jax.experimental.pallas import tpu as pltpu
from jax.sharding import PartitionSpec as P

MESH = pl.DeviceIdType.MESH
SPLITS = 4
DIRECT = 2
HOP = 2
VMEM_MIB = 56


def prefix(x, axis, combine, identity):
    peers, mine = (lax.axis_size(axis), lax.axis_index(axis))
    everything = lax.all_gather(x, axis)
    start = jnp.broadcast_to(jnp.asarray(identity, x.dtype), x.shape)

    def lap(k, before):
        at = peers - 1 - k
        reached = at > mine
        new = combine(before, everything[at])
        return jnp.where(reached, new, before)

    return lax.fori_loop(0, peers, lap, start)


def from_behind(value, axis, steps):
    count = lax.axis_size(axis)
    initial, last = (max(0, -steps), min(count, count - steps))
    return lax.ppermute(value, axis, [(source, source + steps) for source in range(initial, last)])


def complex_product(left_side, right_side, pattern, stack_axis):
    left_real = left_side[:, :, 0]
    left_imag = left_side[:, :, 1]
    right_real = right_side[:, :, 0]
    right_imag = right_side[:, :, 1]
    real_part = jnp.einsum(
        pattern, left_real, right_real, preferred_element_type=jnp.float32
    ) - jnp.einsum(pattern, left_imag, right_imag, preferred_element_type=jnp.float32)
    imag_part = jnp.einsum(
        pattern, left_real, right_imag, preferred_element_type=jnp.float32
    ) + jnp.einsum(pattern, left_imag, right_real, preferred_element_type=jnp.float32)
    return jnp.stack([real_part, imag_part], axis=stack_axis)


def add_pair(earlier, later):
    return earlier + later


def shards(recorded, vertical):
    local_depths = recorded.shape[1]
    row_count = recorded.shape[3]
    depth_cells = lax.axis_size("depth") * local_depths
    depth_step = 1.0 / depth_cells
    first_row = lax.axis_index("col") * row_count
    row_wave = lax.dynamic_slice_in_dim(vertical, first_row, row_count, 1)
    depth_f = (
        lax.axis_index("depth") * local_depths + jnp.arange(local_depths, dtype=jnp.int32)
    ).astype(jnp.float32)
    phase_angle = (row_wave[:, None, :, None] + vertical[:, None, None, :]) * depth_f[
        None, :, None, None
    ]
    cosine = jnp.cos(phase_angle)
    sine_part = jnp.sin(phase_angle)
    real_in = recorded[:, :, 0].astype(jnp.float32)
    imag_in = recorded[:, :, 1].astype(jnp.float32)
    plus32 = (
        jnp.stack(
            [real_in * cosine - imag_in * sine_part, real_in * sine_part + imag_in * cosine], axis=2
        )
        * depth_step
    )
    minus_phase = (
        jnp.stack(
            [real_in * cosine + imag_in * sine_part, imag_in * cosine - real_in * sine_part], axis=2
        )
        * depth_step
    ).astype(jnp.bfloat16)
    inner_sum = lax.cumsum(plus32, axis=1, reverse=True)
    beyond = prefix(inner_sum[:, 0], "depth", add_pair, jnp.zeros_like(inner_sum[:, 0]))
    suffix_all = inner_sum + beyond[:, None]
    following = from_behind(suffix_all[:, 0], "depth", -1)
    tail_sum = jnp.concatenate([suffix_all[:, 1:], following[:, None]], axis=1).astype(jnp.bfloat16)
    columns = tail_sum
    middle = complex_product(
        columns, lax.all_gather(minus_phase, "col", axis=3, tiled=True), "wzrk,wzkc->wzrc", 2
    ).astype(jnp.bfloat16)
    columns = middle
    partial_pred = complex_product(
        columns, lax.all_gather(tail_sum, "col", axis=3, tiled=True), "wzrk,wzkc->wrc", 1
    )
    return lax.psum_scatter(partial_pred, "depth", scatter_dimension=3, tiled=True)


def kernel(
    sizes, rec, vertical, out, waves, table, ct, rt, land, ml, tl, ts, prod, suf, sbuf, srecv, ein, eout, xsend, xrecv,
    dsend, drecv, deep, pacc, psend, precv, fsend, frecv, mine32,
    v_sem, a_send, a_recv, s_send, s_recv, e_send, e_recv, x_send, x_recv, d_send, d_recv, p_send, p_recv,
    q_recv, f_send, f_recv, ready,
):
    levels, freqs, cols, local, rows, size, width, splits, direct = sizes
    depth, col = lax.axis_index("depth"), lax.axis_index("col")
    z, x = depth // 2, depth % 2
    y, core = col // 2, col % 2
    rings = cols // 2
    tiles = 2 * rings
    pieces = size // width * splits
    chained = pieces - direct
    sub = rows // splits
    share_rows = cols * sub // 2
    block = 2 * width
    me = y * 2 + x
    f32, bf16 = jnp.float32, jnp.bfloat16

    def device(zz, xx, yy, cc):
        return (zz * 2 + xx, yy * 2 + cc)

    other_core = device(z, x, y, 1 - core)
    fetch = pltpu.make_async_copy(vertical, waves, v_sem)
    fetch.start()
    barrier = pltpu.get_barrier_semaphore()
    greeted = 0
    for dz in range(1, levels):
        pl.semaphore_signal(
            barrier, inc=1, device_id=(((z + dz) % levels) * 2 + x, col), device_id_type=MESH
        )
        greeted += 1
    for dx in (1, 0):
        for dc in reversed(range(cols)):
            if dx or dc:
                pl.semaphore_signal(
                    barrier, inc=1,
                    device_id=(z * 2 + (x + dx) % 2, (col + dc) % cols), device_id_type=MESH,
                )
                greeted += 1
    pl.semaphore_wait(barrier, greeted)

    def remote(src, dst, send, recv, to):
        return pltpu.make_async_remote_copy(
            src_ref=src, dst_ref=dst, send_sem=send, recv_sem=recv, device_id=to, device_id_type=MESH
        )

    def aligned(i, unit):
        return pl.multiple_of(i * unit, unit)

    def spread(n, dx, dy, near=False):
        j, r = n // splits, n % splits
        xx, yy = (x + dx) % 2, (y + dy) % rings
        lanes = pl.ds(j * width, width)
        src = rec.at[yy * 2 + xx, :, :, pl.ds(r * sub, sub), lanes]
        dst = land.at[:, :, col, pl.ds(r * sub, sub), lanes]
        if near:
            return pltpu.make_async_copy(src, dst, a_recv.at[n])
        return remote(src, dst, a_send, a_recv.at[n], device(z, xx, yy, x))

    routes = [(dx, dy) for dy in reversed(range(rings)) for dx in (1, 0)]
    for n in range(pieces):
        for dx, dy in routes:
            if dx or dy:
                spread(n, dx, dy).start()
            else:
                pl.when(core == x)(lambda: spread(n, dx, dy, near=True).start())
                pl.when(core != x)(lambda: spread(n, dx, dy).start())

    for dz in range(1, levels):
        pl.semaphore_signal(
            ready, inc=1, device_id=(((z + dz) % levels) * 2 + x, col), device_id_type=MESH
        )

    @pl.when(z == levels - 1)
    def _():
        deep[...] = jnp.zeros_like(deep)

    fetch.wait()
    wave = waves[pl.ds(me, 1), :]
    table[...] = jnp.zeros_like(table)
    for l in range(local):
        angle = wave * ((z * 2 + core) * local + l).astype(f32)
        table[2 * l : 2 * l + 1, :] = jnp.cos(angle)
        table[2 * l + 1 : 2 * l + 2, :] = jnp.sin(angle)
    ct[...] = table[...].T
    rt[...] = table[0 : 2 * local, :] * (1.0 / (2 * levels * local))

    def place(n):
        return n // splits, pl.multiple_of(n % splits * sub, sub), pl.ds(aligned(n // splits, width), width)

    def share(n):
        theirs = pl.ds(aligned(1 - core, share_rows), share_rows)
        return remote(sbuf.at[n, :, theirs, :], srecv.at[n], s_send, s_recv.at[n], other_core)

    def down(n):
        to = device((z + levels - 1) % levels, x, y, core)
        return remote(eout.at[n], ein.at[n], e_send, e_recv.at[n], to)

    def leap(i, source, target):
        return remote(
            dsend.at[i], drecv.at[i, source], d_send.at[i, target], d_recv.at[i, source],
            device(target, x, y, core),
        )

    def across(n):
        return remote(xsend.at[n], xrecv.at[n], x_send, x_recv.at[n], other_core)

    def phase(n):
        j, first, lanes = place(n)
        piece = pl.ds(first, sub)
        dst = land.at[:, :, :, piece, lanes]
        pltpu.make_async_copy(dst, dst, a_recv.at[n]).wait()
        shifted = pl.ds(pl.multiple_of(size + j * width, width), width)

        @pl.loop(0, cols)
        def _(t):
            at = pl.ds(pl.multiple_of(t * rows + first, sub), sub)
            mid = pl.multiple_of(t // 2 * 2 * block + t % 2 * rows + first, sub)
            top, low = pl.ds(mid, sub), pl.ds(mid + block, sub)
            sum_re = sum_im = None
            for l in reversed(range(local)):
                if sum_re is not None:
                    suf[l, 0, at, lanes] = sum_re
                    suf[l, 1, at, lanes] = sum_im
                re = land[l, 0, t, piece, lanes].astype(f32)
                im = land[l, 1, t, piece, lanes].astype(f32)
                row_cos, row_sin = ct[at, 2 * l : 2 * l + 1], ct[at, 2 * l + 1 : 2 * l + 2]
                col_cos, col_sin = rt[2 * l : 2 * l + 1, lanes], rt[2 * l + 1 : 2 * l + 2, lanes]
                cosine = row_cos * col_cos - row_sin * col_sin
                sine = row_sin * col_cos + row_cos * col_sin
                a, b, c, d = re * cosine, im * sine, re * sine, im * cosine
                minus_re, minus_im = a + b, d - c
                ml[l, top, lanes] = minus_re.astype(bf16)
                ml[l, low, shifted] = minus_re.astype(bf16)
                ml[l, top, shifted] = (-minus_im).astype(bf16)
                ml[l, low, lanes] = minus_im.astype(bf16)
                plus_re, plus_im = a - b, c + d
                sum_re = plus_re if sum_re is None else sum_re + plus_re
                sum_im = plus_im if sum_im is None else sum_im + plus_im
            packed = pl.ds(aligned(t, sub), sub)
            sbuf[n, 0, packed, :] = sum_re.astype(bf16)
            sbuf[n, 1, packed, :] = sum_im.astype(bf16)

        share(n).start()

    def put_tail(n, half, deeper_at):
        j, first, lanes = place(n)

        @pl.loop(0, cols // 2)
        def _(t):
            deeper = deeper_at(pl.ds(aligned(t, sub), sub))
            start = pl.multiple_of((half * (cols // 2) + t) * rows + first, sub)
            at, low = pl.ds(start, sub), pl.ds(start + size, sub)
            for l in range(local):
                re, im = deeper
                if l < local - 1:
                    re, im = re + suf[l, 0, at, lanes], im + suf[l, 1, at, lanes]
                base = (j // 2 * local + l) * 2 * block + j % 2 * width
                fore = pl.ds(pl.multiple_of(base, width), width)
                back = pl.ds(pl.multiple_of(base + block, width), width)
                ts[l, at, lanes] = re.astype(bf16)
                ts[l, low, lanes] = im.astype(bf16)
                tl[at, fore] = re.astype(bf16)
                tl[low, back] = re.astype(bf16)
                tl[at, back] = (-im).astype(bf16)
                tl[low, fore] = im.astype(bf16)

    def each(step):
        @pl.loop(0, cols // 2)
        def _(t):
            at = pl.ds(aligned(t, sub), sub)
            mine = pl.ds(pl.multiple_of(core * share_rows + t * sub, sub), sub)
            for part in range(2):
                step(part, at, mine)

    def chain(n):
        share(n).wait_recv()

        @pl.when((n < chained) & (z < levels - 1))
        def _():
            down(n).wait_recv()
            deep[...] = ein[n].astype(f32)

        @pl.when((n < chained) & (z > 0))
        def _():
            def hop(part, at, mine):
                own = sbuf[n, part, mine, :].astype(f32)
                their = srecv[n, part, at, :].astype(f32)
                eout[n, part, at, :] = (deep[part, at, :] + own + their).astype(bf16)

            each(hop)
            down(n).start()

        if direct:
            i = n - chained

            @pl.when((n >= chained) & (z > 0))
            def _():
                def total(part, at, mine):
                    own = sbuf[n, part, mine, :].astype(f32)
                    their = srecv[n, part, at, :].astype(f32)
                    dsend[i, part, at, :] = (own + their).astype(bf16)

                each(total)
                for target in range(levels - 1):
                    pl.when(target < z)(lambda: leap(i, z, target).start())

            @pl.when(n >= chained)
            def _():
                for source in range(1, levels):
                    @pl.when(source > z)
                    def _():
                        leap(i, source, z).wait_recv()
                        got = drecv[i, source].astype(f32)

                        @pl.when(source == z + 1)
                        def _():
                            deep[...] = got

                        @pl.when(source > z + 1)
                        def _():
                            deep[...] += got

        def aside(part, at, mine):
            own = sbuf[n, part, mine, :].astype(f32)
            xsend[n, part, at, :] = (deep[part, at, :] + jnp.where(core == 1, own, 0.0)).astype(bf16)

        each(aside)
        across(n).start()

        def deeper(at):
            return [
                deep[part, at, :] + jnp.where(core == 0, srecv[n, part, at, :].astype(f32), 0.0)
                for part in range(2)
            ]

        put_tail(n, core, deeper)

    def finish(n):
        across(n).wait_recv()
        put_tail(n, 1 - core, lambda at: [xrecv[n, part, at, :].astype(f32) for part in range(2)])

    span = local * 2 * block

    def middle(h):
        lanes = slice(h * block, (h + 1) * block)
        for l in range(local):
            result = jnp.dot(ml[l], ts[l, :, lanes], preferred_element_type=f32).astype(bf16)
            for half in range(2):
                base = half * span + l * 2 * block
                prod[base : base + 2 * block, lanes] = result[half * 2 * block : (half + 1) * 2 * block]

    def outer(h, begin, end):
        lanes = slice(h * block, (h + 1) * block)
        result = jnp.dot(tl[:, begin:end], prod[begin:end, lanes], preferred_element_type=f32)
        return result.reshape(tiles, 2, rows, block)

    lag = 1 + HOP * (levels - 1 - z)

    steps = pieces + HOP * (levels - 1) + 2
    soon = max(pieces - 1, 1 + HOP * (levels - 1) + pieces // 2)
    ripe = jnp.where(z == 0, soon, steps - 1)

    @pl.loop(0, steps)
    def _(s):
        pl.when(s < pieces)(lambda: phase(s))
        c = s - lag
        pl.when((c >= 0) & (c < pieces))(lambda: chain(c))
        f = c - 1
        pl.when((f >= 0) & (f < pieces))(lambda: finish(f))

        @pl.when(s == ripe)
        def _():
            middle(0)
            pacc[0] = outer(0, 0, span)

    def pair(h):
        return remote(psend.at[h], precv.at[h], p_send, p_recv.at[h], other_core)

    def swap(h):
        @pl.loop(0, tiles)
        def _(t):
            psend[h, t] = pacc[h, t, 1 - core].astype(bf16)

        pair(h).start()

    def low_block():
        pacc[0] += outer(0, span, 2 * span)
        swap(0)

    def high_block():
        pacc[1] = outer(1, 0, 2 * span)
        swap(1)

    middle(1)

    @pl.when(z < levels // 2)
    def _():
        high_block()
        low_block()

    @pl.when(z >= levels // 2)
    def _():
        low_block()
        high_block()

    narrow = width // 2

    def owner(target, dx, dy):
        xx, yy = (x + dx) % 2, (y + dy) % rings
        return remote(
            fsend.at[target * freqs + yy * 2 + xx], frecv.at[z, me], f_send, q_recv.at[z],
            device(target, xx, yy, core),
        )

    def neighbour(dx, dy):
        xx, yy = (x + dx) % 2, (y + dy) % rings
        return remote(
            fsend.at[z * freqs + yy * 2 + xx], frecv.at[z, me], f_send, f_recv.at[me],
            device(z, xx, yy, core),
        )

    def ship(h, s):
        target = h * 2 + s
        lanes = pl.ds(aligned(s, width), width)
        for yy in range(rings):
            re, im = [
                pacc[h, part * rings + yy, core, :, lanes]
                + precv[h, part * rings + yy, :, lanes].astype(f32)
                for part in range(2)
            ]
            for xx in range(2):
                cut = slice(xx * narrow, (xx + 1) * narrow)
                joined = jnp.concatenate([re[:, cut], im[:, cut]], axis=1)
                fsend[target * freqs + yy * 2 + xx] = joined.astype(bf16)

                @pl.when(target == z)
                def _():
                    mine32[yy, xx] = joined

        @pl.when(target == z)
        def _():
            for dx, dy in routes:
                if dx or dy:
                    neighbour(dx, dy).start()

        @pl.when(target != z)
        def _():
            for dx, dy in routes:
                owner(target, dx, dy).start()

    pl.semaphore_wait(ready, levels - 1)
    far = 1 - z // 2
    toward = jnp.where(z < levels // 2, 1, 0)
    pair(far).wait_recv()
    ship(far, toward)
    ship(far, 1 - toward)
    pair(1 - far).wait_recv()
    ship(1 - far, 1 - z % 2)
    ship(1 - far, z % 2)

    out[me] = mine32[y, x]
    for dx, dy in reversed(routes):
        if dx or dy:
            w = (y + dy) % rings * 2 + (x + dx) % 2
            pltpu.make_async_copy(frecv.at[z, w], frecv.at[z, w], f_recv.at[w]).wait()
            out[w] = frecv[z, w].astype(f32)

    for source in reversed(range(levels)):
        @pl.when(source != z)
        def _():
            pltpu.make_async_copy(frecv.at[source], frecv.at[source], q_recv.at[source]).wait()
            out[...] += frecv[source].astype(f32)

    def sent(ref, sem):
        pltpu.make_async_copy(ref, ref, sem).wait()

    pl.when(core == x)(lambda: sent(rec.at[pl.ds(0, freqs - 1)], a_send))
    pl.when(core != x)(lambda: sent(rec, a_send))
    sent(sbuf.at[:, :, pl.ds(0, share_rows), :], s_send)
    pl.when(z > 0)(lambda: sent(eout, e_send))
    sent(xsend, x_send)
    for i in range(direct):
        for target in range(levels - 1):
            pl.when(target < z)(lambda: leap(i, z, target).wait_send())
    sent(psend, p_send)
    sent(fsend.at[pl.ds(0, levels * freqs - 1)], f_send)


def fused(recorded, vertical):
    freqs, local, _, rows, size = recorded.shape
    depths, cols = lax.axis_size("depth"), lax.axis_size("col")
    levels, width = depths // 2, 2 * size // depths
    tiles = cols
    pieces, share_rows = size // width * SPLITS, rows * cols // SPLITS // 2
    chained, leaps = pieces - DIRECT, max(DIRECT, 1)
    sizes = (levels, freqs, cols, local, rows, size, width, SPLITS, DIRECT)
    f32, bf16 = jnp.float32, jnp.bfloat16
    dma = pltpu.SemaphoreType.DMA
    packed = pl.pallas_call(
        functools.partial(kernel, sizes),
        out_shape=jax.ShapeDtypeStruct((freqs, rows, width), f32),
        in_specs=[
            pl.BlockSpec(memory_space=pl.ANY),
            pl.BlockSpec(memory_space=pl.ANY),
        ],
        out_specs=pl.BlockSpec(memory_space=pltpu.VMEM),
        scratch_shapes=[
            pltpu.VMEM((freqs, size), f32),
            pltpu.VMEM((128, size), f32),
            pltpu.VMEM((size, 128), f32),
            pltpu.VMEM((2 * local, size), f32),
            pltpu.VMEM((local, 2, cols, rows, size), bf16),
            pltpu.VMEM((local, 2 * size, 2 * size), bf16),
            pltpu.VMEM((2 * size, local * 2 * size), bf16),
            pltpu.VMEM((local, 2 * size, size), bf16),
            pltpu.VMEM((local * 2 * size, size), bf16),
            pltpu.VMEM((local - 1, 2, size, size), f32),
            pltpu.VMEM((pieces, 2, 2 * share_rows, width), bf16),
            pltpu.VMEM((pieces, 2, share_rows, width), bf16),
            pltpu.VMEM((chained, 2, share_rows, width), bf16),
            pltpu.VMEM((chained, 2, share_rows, width), bf16),
            pltpu.VMEM((pieces, 2, share_rows, width), bf16),
            pltpu.VMEM((pieces, 2, share_rows, width), bf16),
            pltpu.VMEM((leaps, 2, share_rows, width), bf16),
            pltpu.VMEM((leaps, levels, 2, share_rows, width), bf16),
            pltpu.VMEM((2, share_rows, width), f32),
            pltpu.VMEM((2, tiles, 2, rows, 2 * width), f32),
            pltpu.VMEM((2, tiles, rows, 2 * width), bf16),
            pltpu.VMEM((2, tiles, rows, 2 * width), bf16),
            pltpu.VMEM((levels * freqs, rows, width), bf16),
            pltpu.VMEM((levels, freqs, rows, width), bf16),
            pltpu.VMEM((cols // 2, 2, rows, width), f32),
            dma, dma, dma((pieces,)),
            dma, dma((pieces,)),
            dma, dma((chained,)),
            dma, dma((pieces,)),
            dma((leaps, levels - 1)), dma((leaps, levels)),
            dma, dma((2,)),
            dma((levels,)), dma, dma((freqs,)),
            pltpu.SemaphoreType.REGULAR,
        ],
        compiler_params=pltpu.CompilerParams(
            collective_id=0, has_side_effects=True, vmem_limit_bytes=VMEM_MIB * 1024 * 1024
        ),
        name="prediction",
    )(recorded, vertical)
    return packed.reshape(freqs, rows, 2, width // 2).transpose(0, 2, 1, 3)


def body(recorded, vertical):
    freqs, local, _, rows, size = recorded.shape
    depths, cols = lax.axis_size("depth"), lax.axis_size("col")
    fits = cols == freqs and cols % 2 == 0 and depths % 4 == 0 and local > 1
    fits = fits and rows % 128 == 0 and depths == 8 and 2 * size // depths == rows
    return fused(recorded, vertical) if fits else shards(recorded, vertical)


def solution(mesh):
    in_specs = (P(None, "depth", None, "col", None), P())
    out_specs = P(None, None, "col", "depth")
    return jax.shard_map(body, mesh=mesh, in_specs=in_specs, out_specs=out_specs, check_vma=False)
```

time: 68.3 us -> 62.5 us (0.915)
  the two profiles are of different devices: /device:TPU:8 before, /device:TPU:16 now
where the time goes in v1:
time: 62.5 us; the launch traced here: 62.4 us
  Pallas kernels  60.6 us (97%)
  local copies, waits for them, and re-layouts  1.79 us (3%)
    pallas_call x1, Pallas kernels, fused(): pl.pallas_call(functools.partial(kernel, sizes), out_shape=jax.ShapeDtype...  60.6 us
    pallas_call x1, local copies, waits for them, and re-layouts, fused(): pl.pallas_call(functools.partial(kernel, sizes), out_shape=jax.ShapeDtype...  1.79 us

profile of v1, /device:TPU:16, one launch (start us, length us, event | category | flops | bytes accessed | tf_op | source)
XLA Modules:
  0.0 62.4 jit_solution(7596967174532325007)
XLA Ops:
  0.0 60.6 %prediction.1 = f32[4,128,128]{2,1,0:T(8,128)} custom-call(bf16[4,2,2,128,512]{4,3,2,1,0:T(8,128)(2,1)} %rec.1, f32[4,512]{1,0:T(4,128)} %vertical.1), custom_call_target="tpu_custom_call" | custom-call | tf_op jit(solution)/shard_map/prediction/pallas_call | solution.py:501
  60.6 1.8 %copy.4 = f32[4,128,128]{1,2,0:T(8,128)} copy(f32[4,128,128]{2,1,0:T(8,128)} %prediction.1) | data formatting | bytes 524288 | tf_op jit(solution)/shard_map/prediction/pallas_call | solution.py:501

commit v2 on v1

--- a/solution.py
+++ b/solution.py
@@ -9,7 +9,6 @@
 
 MESH = pl.DeviceIdType.MESH
 SPLITS = 4
-DIRECT = 2
 HOP = 2
 VMEM_MIB = 56
 
@@ -99,18 +98,18 @@
 
 def kernel(
     sizes, rec, vertical, out, waves, table, ct, rt, land, ml, tl, ts, prod, suf, sbuf, srecv, ein, eout, xsend, xrecv,
-    dsend, drecv, deep, pacc, psend, precv, fsend, frecv, mine32,
-    v_sem, a_send, a_recv, s_send, s_recv, e_send, e_recv, x_send, x_recv, d_send, d_recv, p_send, p_recv,
+    stage, presend, keep, deep, pacc, psend, precv, fsend, frecv, mine32,
+    v_sem, a_send, a_recv, s_send, s_recv, e_send, e_recv, x_send, x_recv, g_sem, g_send, g_recv, p_send, p_recv,
     q_recv, f_send, f_recv, ready,
 ):
-    levels, freqs, cols, local, rows, size, width, splits, direct = sizes
+    levels, freqs, cols, local, rows, size, width, splits = sizes
     depth, col = lax.axis_index("depth"), lax.axis_index("col")
     z, x = depth // 2, depth % 2
     y, core = col // 2, col % 2
     rings = cols // 2
     tiles = 2 * rings
     pieces = size // width * splits
-    chained = pieces - direct
+    plain = pieces - splits
     sub = rows // splits
     share_rows = cols * sub // 2
     block = 2 * width
@@ -123,6 +122,9 @@
     other_core = device(z, x, y, 1 - core)
     fetch = pltpu.make_async_copy(vertical, waves, v_sem)
     fetch.start()
+    last = pl.ds(size - width, width)
+    local_last = pltpu.make_async_copy(rec.at[:, :, :, :, last], stage, g_sem)
+    local_last.start()
     barrier = pltpu.get_barrier_semaphore()
     greeted = 0
     for dz in range(1, levels):
@@ -138,6 +140,44 @@
                     device_id=(z * 2 + (x + dx) % 2, (col + dc) % cols), device_id_type=MESH,
                 )
                 greeted += 1
+
+    fetch.wait()
+    wave = waves[pl.ds(me, 1), :]
+    every = waves[...]
+    table[...] = jnp.zeros_like(table)
+    own = 4 * local
+    for l in range(local):
+        angle = wave * ((z * 2 + core) * local + l).astype(f32)
+        table[2 * l : 2 * l + 1, :] = jnp.cos(angle)
+        table[2 * l + 1 : 2 * l + 2, :] = jnp.sin(angle)
+        angle = every * (depth * local + l).astype(f32)
+        base = own + 2 * l * freqs
+        table[base : base + freqs, :] = jnp.cos(angle)
+        table[base + freqs : base + 2 * freqs, :] = jnp.sin(angle)
+    ct[...] = table[...].T
+    rt[...] = table[0 : own + 2 * local * freqs, :] * (1.0 / (2 * levels * local))
+    local_last.wait()
+
+    @pl.loop(0, splits)
+    def _(r):
+        at = pl.ds(pl.multiple_of(r * sub, sub), sub)
+        line = pl.ds(pl.multiple_of(col * rows + r * sub, sub), sub)
+        for w in range(freqs):
+            sum_re = sum_im = None
+            for l in range(local):
+                c = own + 2 * l * freqs + w
+                d = c + freqs
+                re, im = stage[w, l, 0, at, :].astype(f32), stage[w, l, 1, at, :].astype(f32)
+                row_cos, row_sin = ct[line, c : c + 1], ct[line, d : d + 1]
+                col_cos, col_sin = rt[c : c + 1, last], rt[d : d + 1, last]
+                cosine = row_cos * col_cos - row_sin * col_sin
+                sine = row_sin * col_cos + row_cos * col_sin
+                plus_re, plus_im = re * cosine - im * sine, re * sine + im * cosine
+                sum_re = plus_re if sum_re is None else sum_re + plus_re
+                sum_im = plus_im if sum_im is None else sum_im + plus_im
+            presend[w, r, 0] = sum_re.astype(bf16)
+            presend[w, r, 1] = sum_im.astype(bf16)
+
     pl.semaphore_wait(barrier, greeted)
 
     def remote(src, dst, send, recv, to):
@@ -158,7 +198,21 @@
             return pltpu.make_async_copy(src, dst, a_recv.at[n])
         return remote(src, dst, a_send, a_recv.at[n], device(z, xx, yy, x))
 
+    def early(dx, dy, near=False):
+        xx, yy = (x + dx) % 2, (y + dy) % rings
+        src = presend.at[yy * 2 + xx]
+        dst = sbuf.at[pl.ds(plain, splits), :, pl.ds(pl.multiple_of(col * sub, sub), sub), :]
+        if near:
+            return pltpu.make_async_copy(src, dst, g_recv)
+        return remote(src, dst, g_send, g_recv, device(z, xx, yy, x))
+
     routes = [(dx, dy) for dy in reversed(range(rings)) for dx in (1, 0)]
+    for dx, dy in routes:
+        if dx or dy:
+            early(dx, dy).start()
+        else:
+            pl.when(core == x)(lambda: early(dx, dy, near=True).start())
+            pl.when(core != x)(lambda: early(dx, dy).start())
     for n in range(pieces):
         for dx, dy in routes:
             if dx or dy:
@@ -176,16 +230,6 @@
     def _():
         deep[...] = jnp.zeros_like(deep)
 
-    fetch.wait()
-    wave = waves[pl.ds(me, 1), :]
-    table[...] = jnp.zeros_like(table)
-    for l in range(local):
-        angle = wave * ((z * 2 + core) * local + l).astype(f32)
-        table[2 * l : 2 * l + 1, :] = jnp.cos(angle)
-        table[2 * l + 1 : 2 * l + 2, :] = jnp.sin(angle)
-    ct[...] = table[...].T
-    rt[...] = table[0 : 2 * local, :] * (1.0 / (2 * levels * local))
-
     def place(n):
         return n // splits, pl.multiple_of(n % splits * sub, sub), pl.ds(aligned(n // splits, width), width)
 
@@ -196,12 +240,6 @@
     def down(n):
         to = device((z + levels - 1) % levels, x, y, core)
         return remote(eout.at[n], ein.at[n], e_send, e_recv.at[n], to)
-
-    def leap(i, source, target):
-        return remote(
-            dsend.at[i], drecv.at[i, source], d_send.at[i, target], d_recv.at[i, source],
-            device(target, x, y, core),
-        )
 
     def across(n):
         return remote(xsend.at[n], xrecv.at[n], x_send, x_recv.at[n], other_core)
@@ -238,11 +276,14 @@
                 plus_re, plus_im = a - b, c + d
                 sum_re = plus_re if sum_re is None else sum_re + plus_re
                 sum_im = plus_im if sum_im is None else sum_im + plus_im
-            packed = pl.ds(aligned(t, sub), sub)
-            sbuf[n, 0, packed, :] = sum_re.astype(bf16)
-            sbuf[n, 1, packed, :] = sum_im.astype(bf16)
-
-        share(n).start()
+
+            @pl.when(n < plain)
+            def _():
+                packed = pl.ds(aligned(t, sub), sub)
+                sbuf[n, 0, packed, :] = sum_re.astype(bf16)
+                sbuf[n, 1, packed, :] = sum_im.astype(bf16)
+
+        pl.when(n < plain)(lambda: share(n).start())
 
     def put_tail(n, half, deeper_at):
         j, first, lanes = place(n)
@@ -274,15 +315,15 @@
             for part in range(2):
                 step(part, at, mine)
 
-    def chain(n):
+    def chain(n, ahead=False):
         share(n).wait_recv()
 
-        @pl.when((n < chained) & (z < levels - 1))
+        @pl.when(z < levels - 1)
         def _():
             down(n).wait_recv()
             deep[...] = ein[n].astype(f32)
 
-        @pl.when((n < chained) & (z > 0))
+        @pl.when(z > 0)
         def _():
             def hop(part, at, mine):
                 own = sbuf[n, part, mine, :].astype(f32)
@@ -292,36 +333,6 @@
             each(hop)
             down(n).start()
 
-        if direct:
-            i = n - chained
-
-            @pl.when((n >= chained) & (z > 0))
-            def _():
-                def total(part, at, mine):
-                    own = sbuf[n, part, mine, :].astype(f32)
-                    their = srecv[n, part, at, :].astype(f32)
-                    dsend[i, part, at, :] = (own + their).astype(bf16)
-
-                each(total)
-                for target in range(levels - 1):
-                    pl.when(target < z)(lambda: leap(i, z, target).start())
-
-            @pl.when(n >= chained)
-            def _():
-                for source in range(1, levels):
-                    @pl.when(source > z)
-                    def _():
-                        leap(i, source, z).wait_recv()
-                        got = drecv[i, source].astype(f32)
-
-                        @pl.when(source == z + 1)
-                        def _():
-                            deep[...] = got
-
-                        @pl.when(source > z + 1)
-                        def _():
-                            deep[...] += got
-
         def aside(part, at, mine):
             own = sbuf[n, part, mine, :].astype(f32)
             xsend[n, part, at, :] = (deep[part, at, :] + jnp.where(core == 1, own, 0.0)).astype(bf16)
@@ -329,17 +340,24 @@
         each(aside)
         across(n).start()
 
-        def deeper(at):
-            return [
-                deep[part, at, :] + jnp.where(core == 0, srecv[n, part, at, :].astype(f32), 0.0)
-                for part in range(2)
-            ]
-
-        put_tail(n, core, deeper)
+        def deeper(part, at):
+            return deep[part, at, :] + jnp.where(core == 0, srecv[n, part, at, :].astype(f32), 0.0)
+
+        def hold(part, at, mine):
+            keep[n - plain, part, at, :] = deeper(part, at)
+
+        if ahead:
+            each(hold)
+        else:
+            put_tail(n, core, lambda at: [deeper(part, at) for part in range(2)])
 
     def finish(n):
         across(n).wait_recv()
         put_tail(n, 1 - core, lambda at: [xrecv[n, part, at, :].astype(f32) for part in range(2)])
+
+    def held(n):
+        put_tail(n, core, lambda at: [keep[n - plain, part, at, :] for part in range(2)])
+        finish(n)
 
     span = local * 2 * block
 
@@ -356,19 +374,24 @@
         result = jnp.dot(tl[:, begin:end], prod[begin:end, lanes], preferred_element_type=f32)
         return result.reshape(tiles, 2, rows, block)
 
-    lag = 1 + HOP * (levels - 1 - z)
-
-    steps = pieces + HOP * (levels - 1) + 2
-    soon = max(pieces - 1, 1 + HOP * (levels - 1) + pieces // 2)
-    ripe = jnp.where(z == 0, soon, steps - 1)
-
-    @pl.loop(0, steps)
+    pltpu.make_async_copy(
+        sbuf.at[pl.ds(plain, splits)], sbuf.at[pl.ds(plain, splits)], g_recv
+    ).wait()
+    for i in range(splits):
+        share(plain + i).start()
+    above = HOP * (levels - 1 - z)
+    ripe = jnp.where(z == 0, pieces - 1, jnp.maximum(pieces - 1, plain + above))
+
+    @pl.loop(0, max(pieces, plain + 2 + HOP * (levels - 1)))
     def _(s):
         pl.when(s < pieces)(lambda: phase(s))
-        c = s - lag
-        pl.when((c >= 0) & (c < pieces))(lambda: chain(c))
+        c = s - above - 1
+        pl.when((c >= 0) & (c < plain))(lambda: chain(c))
+        e = s - above
+        pl.when((e >= 0) & (e < splits))(lambda: chain(plain + e, True))
         f = c - 1
-        pl.when((f >= 0) & (f < pieces))(lambda: finish(f))
+        pl.when((f >= 0) & (f < plain))(lambda: finish(f))
+        pl.when((s >= plain) & (s < pieces))(lambda: held(s))
 
         @pl.when(s == ripe)
         def _():
@@ -481,9 +504,8 @@
     sent(sbuf.at[:, :, pl.ds(0, share_rows), :], s_send)
     pl.when(z > 0)(lambda: sent(eout, e_send))
     sent(xsend, x_send)
-    for i in range(direct):
-        for target in range(levels - 1):
-            pl.when(target < z)(lambda: leap(i, z, target).wait_send())
+    pl.when(core == x)(lambda: sent(presend.at[pl.ds(0, freqs - 1)], g_send))
+    pl.when(core != x)(lambda: sent(presend, g_send))
     sent(psend, p_send)
     sent(fsend.at[pl.ds(0, levels * freqs - 1)], f_send)
 
@@ -494,8 +516,7 @@
     levels, width = depths // 2, 2 * size // depths
     tiles = cols
     pieces, share_rows = size // width * SPLITS, rows * cols // SPLITS // 2
-    chained, leaps = pieces - DIRECT, max(DIRECT, 1)
-    sizes = (levels, freqs, cols, local, rows, size, width, SPLITS, DIRECT)
+    sizes = (levels, freqs, cols, local, rows, size, width, SPLITS)
     f32, bf16 = jnp.float32, jnp.bfloat16
     dma = pltpu.SemaphoreType.DMA
     packed = pl.pallas_call(
@@ -510,7 +531,7 @@
             pltpu.VMEM((freqs, size), f32),
             pltpu.VMEM((128, size), f32),
             pltpu.VMEM((size, 128), f32),
-            pltpu.VMEM((2 * local, size), f32),
+            pltpu.VMEM((local * (4 + 2 * freqs), size), f32),
             pltpu.VMEM((local, 2, cols, rows, size), bf16),
             pltpu.VMEM((local, 2 * size, 2 * size), bf16),
             pltpu.VMEM((2 * size, local * 2 * size), bf16),
@@ -519,12 +540,13 @@
             pltpu.VMEM((local - 1, 2, size, size), f32),
             pltpu.VMEM((pieces, 2, 2 * share_rows, width), bf16),
             pltpu.VMEM((pieces, 2, share_rows, width), bf16),
-            pltpu.VMEM((chained, 2, share_rows, width), bf16),
-            pltpu.VMEM((chained, 2, share_rows, width), bf16),
             pltpu.VMEM((pieces, 2, share_rows, width), bf16),
             pltpu.VMEM((pieces, 2, share_rows, width), bf16),
-            pltpu.VMEM((leaps, 2, share_rows, width), bf16),
-            pltpu.VMEM((leaps, levels, 2, share_rows, width), bf16),
+            pltpu.VMEM((pieces, 2, share_rows, width), bf16),
+            pltpu.VMEM((pieces, 2, share_rows, width), bf16),
+            pltpu.VMEM((freqs, local, 2, rows, width), bf16),
+            pltpu.VMEM((freqs, SPLITS, 2, rows // SPLITS, width), bf16),
+            pltpu.VMEM((SPLITS, 2, share_rows, width), f32),
             pltpu.VMEM((2, share_rows, width), f32),
             pltpu.VMEM((2, tiles, 2, rows, 2 * width), f32),
             pltpu.VMEM((2, tiles, rows, 2 * width), bf16),
@@ -534,9 +556,9 @@
             pltpu.VMEM((cols // 2, 2, rows, width), f32),
             dma, dma, dma((pieces,)),
             dma, dma((pieces,)),
-            dma, dma((chained,)),
             dma, dma((pieces,)),
-            dma((leaps, levels - 1)), dma((leaps, levels)),
+            dma, dma((pieces,)),
+            dma, dma, dma,
             dma, dma((2,)),
             dma((levels,)), dma, dma((freqs,)),
             pltpu.SemaphoreType.REGULAR,

time: 62.5 us -> 57.3 us (0.917)
  the two profiles are of different devices: /device:TPU:16 before, /device:TPU:0 now
where the time goes in v2:
time: 57.3 us; the launch traced here: 56.7 us
  Pallas kernels  54.9 us (96%)
  local copies, waits for them, and re-layouts  1.79 us (3%)
    pallas_call x1, Pallas kernels, fused(): pl.pallas_call(functools.partial(kernel, sizes), out_shape=jax.ShapeDtype...  54.9 us
    pallas_call x1, local copies, waits for them, and re-layouts, fused(): pl.pallas_call(functools.partial(kernel, sizes), out_shape=jax.ShapeDtype...  1.79 us

profile of v2, /device:TPU:0, one launch (start us, length us, event | category | flops | bytes accessed | tf_op | source)
XLA Modules:
  0.0 56.7 jit_solution(12769871517614415693)
XLA Ops:
  0.0 54.9 %prediction.1 = f32[4,128,128]{2,1,0:T(8,128)} custom-call(bf16[4,2,2,128,512]{4,3,2,1,0:T(8,128)(2,1)} %rec.1, f32[4,512]{1,0:T(4,128)} %vertical.1), custom_call_target="tpu_custom_call" | custom-call | tf_op jit(solution)/shard_map/prediction/pallas_call | solution.py:522
  54.9 1.8 %copy.4 = f32[4,128,128]{1,2,0:T(8,128)} copy(f32[4,128,128]{2,1,0:T(8,128)} %prediction.1) | data formatting | bytes 524288 | tf_op jit(solution)/shard_map/prediction/pallas_call | solution.py:522

commit v3 on v2

--- a/solution.py
+++ b/solution.py
@@ -9,7 +9,8 @@
 
 MESH = pl.DeviceIdType.MESH
 SPLITS = 4
-HOP = 2
+HOP = 3
+LEAD = 2
 VMEM_MIB = 56
 
 
@@ -98,9 +99,9 @@
 
 def kernel(
     sizes, rec, vertical, out, waves, table, ct, rt, land, ml, tl, ts, prod, suf, sbuf, srecv, ein, eout, xsend, xrecv,
-    stage, presend, keep, deep, pacc, psend, precv, fsend, frecv, mine32,
+    stage, presend, keep, deep, pacc, psend, precv, fsend, frecv, rrecv, mine32,
     v_sem, a_send, a_recv, s_send, s_recv, e_send, e_recv, x_send, x_recv, g_sem, g_send, g_recv, p_send, p_recv,
-    q_recv, f_send, f_recv, ready,
+    q_recv, r_recv, f_send, f_recv, ready,
 ):
     levels, freqs, cols, local, rows, size, width, splits = sizes
     depth, col = lax.axis_index("depth"), lax.axis_index("col")
@@ -109,7 +110,8 @@
     rings = cols // 2
     tiles = 2 * rings
     pieces = size // width * splits
-    plain = pieces - splits
+    ahead = pieces // 2
+    plain = pieces - ahead
     sub = rows // splits
     share_rows = cols * sub // 2
     block = 2 * width
@@ -119,11 +121,13 @@
     def device(zz, xx, yy, cc):
         return (zz * 2 + xx, yy * 2 + cc)
 
+    def aligned(i, unit):
+        return pl.multiple_of(i * unit, unit)
+
     other_core = device(z, x, y, 1 - core)
     fetch = pltpu.make_async_copy(vertical, waves, v_sem)
     fetch.start()
-    last = pl.ds(size - width, width)
-    local_last = pltpu.make_async_copy(rec.at[:, :, :, :, last], stage, g_sem)
+    local_last = pltpu.make_async_copy(rec.at[:, :, :, :, pl.ds(size // 2, size // 2)], stage, g_sem)
     local_last.start()
     barrier = pltpu.get_barrier_semaphore()
     greeted = 0
@@ -158,16 +162,20 @@
     rt[...] = table[0 : own + 2 * local * freqs, :] * (1.0 / (2 * levels * local))
     local_last.wait()
 
-    @pl.loop(0, splits)
-    def _(r):
+    @pl.loop(0, ahead)
+    def _(i):
+        r = i % splits
         at = pl.ds(pl.multiple_of(r * sub, sub), sub)
+        part_lanes = pl.ds(aligned(i // splits, width), width)
+        last = pl.ds(pl.multiple_of(size // 2 + i // splits * width, width), width)
         line = pl.ds(pl.multiple_of(col * rows + r * sub, sub), sub)
         for w in range(freqs):
             sum_re = sum_im = None
             for l in range(local):
                 c = own + 2 * l * freqs + w
                 d = c + freqs
-                re, im = stage[w, l, 0, at, :].astype(f32), stage[w, l, 1, at, :].astype(f32)
+                re = stage[w, l, 0, at, part_lanes].astype(f32)
+                im = stage[w, l, 1, at, part_lanes].astype(f32)
                 row_cos, row_sin = ct[line, c : c + 1], ct[line, d : d + 1]
                 col_cos, col_sin = rt[c : c + 1, last], rt[d : d + 1, last]
                 cosine = row_cos * col_cos - row_sin * col_sin
@@ -175,8 +183,8 @@
                 plus_re, plus_im = re * cosine - im * sine, re * sine + im * cosine
                 sum_re = plus_re if sum_re is None else sum_re + plus_re
                 sum_im = plus_im if sum_im is None else sum_im + plus_im
-            presend[w, r, 0] = sum_re.astype(bf16)
-            presend[w, r, 1] = sum_im.astype(bf16)
+            presend[w, i, 0] = sum_re.astype(bf16)
+            presend[w, i, 1] = sum_im.astype(bf16)
 
     pl.semaphore_wait(barrier, greeted)
 
@@ -184,9 +192,6 @@
         return pltpu.make_async_remote_copy(
             src_ref=src, dst_ref=dst, send_sem=send, recv_sem=recv, device_id=to, device_id_type=MESH
         )
-
-    def aligned(i, unit):
-        return pl.multiple_of(i * unit, unit)
 
     def spread(n, dx, dy, near=False):
         j, r = n // splits, n % splits
@@ -201,7 +206,7 @@
     def early(dx, dy, near=False):
         xx, yy = (x + dx) % 2, (y + dy) % rings
         src = presend.at[yy * 2 + xx]
-        dst = sbuf.at[pl.ds(plain, splits), :, pl.ds(pl.multiple_of(col * sub, sub), sub), :]
+        dst = sbuf.at[pl.ds(plain, ahead), :, pl.ds(pl.multiple_of(col * sub, sub), sub), :]
         if near:
             return pltpu.make_async_copy(src, dst, g_recv)
         return remote(src, dst, g_send, g_recv, device(z, xx, yy, x))
@@ -315,7 +320,7 @@
             for part in range(2):
                 step(part, at, mine)
 
-    def chain(n, ahead=False):
+    def chain(n, hold_on=False):
         share(n).wait_recv()
 
         @pl.when(z < levels - 1)
@@ -346,7 +351,7 @@
         def hold(part, at, mine):
             keep[n - plain, part, at, :] = deeper(part, at)
 
-        if ahead:
+        if hold_on:
             each(hold)
         else:
             put_tail(n, core, lambda at: [deeper(part, at) for part in range(2)])
@@ -375,28 +380,27 @@
         return result.reshape(tiles, 2, rows, block)
 
     pltpu.make_async_copy(
-        sbuf.at[pl.ds(plain, splits)], sbuf.at[pl.ds(plain, splits)], g_recv
+        sbuf.at[pl.ds(plain, ahead)], sbuf.at[pl.ds(plain, ahead)], g_recv
     ).wait()
-    for i in range(splits):
+    for i in range(ahead):
         share(plain + i).start()
-    above = HOP * (levels - 1 - z)
-    ripe = jnp.where(z == 0, pieces - 1, jnp.maximum(pieces - 1, plain + above))
+    above, soon = HOP * (levels - 1 - z), LEAD * (levels - 1 - z)
 
     @pl.loop(0, max(pieces, plain + 2 + HOP * (levels - 1)))
     def _(s):
         pl.when(s < pieces)(lambda: phase(s))
         c = s - above - 1
         pl.when((c >= 0) & (c < plain))(lambda: chain(c))
-        e = s - above
-        pl.when((e >= 0) & (e < splits))(lambda: chain(plain + e, True))
+        e = s - soon
+        pl.when((e >= 0) & (e < ahead))(lambda: chain(plain + e, True))
         f = c - 1
         pl.when((f >= 0) & (f < plain))(lambda: finish(f))
         pl.when((s >= plain) & (s < pieces))(lambda: held(s))
 
-        @pl.when(s == ripe)
+        @pl.when(s == pieces - 1)
         def _():
-            middle(0)
-            pacc[0] = outer(0, 0, span)
+            middle(1)
+            pacc[1] = outer(1, span, 2 * span)
 
     def pair(h):
         return remote(psend.at[h], precv.at[h], p_send, p_recv.at[h], other_core)
@@ -409,29 +413,32 @@
         pair(h).start()
 
     def low_block():
-        pacc[0] += outer(0, span, 2 * span)
+        pacc[0] = outer(0, 0, 2 * span)
         swap(0)
 
     def high_block():
-        pacc[1] = outer(1, 0, 2 * span)
+        pacc[1] += outer(1, 0, span)
         swap(1)
 
-    middle(1)
-
-    @pl.when(z < levels // 2)
+    middle(0)
+
+    @pl.when(z % 2 == 0)
     def _():
         high_block()
         low_block()
 
-    @pl.when(z >= levels // 2)
+    @pl.when(z % 2 == 1)
     def _():
         low_block()
         high_block()
 
     narrow = width // 2
-
-    def owner(target, dx, dy):
-        xx, yy = (x + dx) % 2, (y + dy) % rings
+    near, far = z // 2, 1 - z // 2
+    toward = jnp.where(z < levels // 2, 1, 0)
+    relay = jnp.where(z == 0, 1, levels - 2)
+    at_end = (z == 0) | (z == levels - 1)
+
+    def owner(target, xx, yy):
         return remote(
             fsend.at[target * freqs + yy * 2 + xx], frecv.at[z, me], f_send, q_recv.at[z],
             device(target, xx, yy, core),
@@ -444,44 +451,66 @@
             device(z, xx, yy, core),
         )
 
-    def ship(h, s):
-        target = h * 2 + s
+    def inward(target, k):
+        return remote(
+            fsend.at[target * freqs + k % freqs], rrecv.at[k], f_send, r_recv.at[k],
+            device(relay, x, y, core),
+        )
+
+    def joined(h, s, yy):
         lanes = pl.ds(aligned(s, width), width)
+        re, im = [
+            pacc[h, part * rings + yy, core, :, lanes]
+            + precv[h, part * rings + yy, :, lanes].astype(f32)
+            for part in range(2)
+        ]
+        cuts = [slice(xx * narrow, (xx + 1) * narrow) for xx in range(2)]
+        return [jnp.concatenate([re[:, cut], im[:, cut]], axis=1) for cut in cuts]
+
+    def ship_far(relayed):
+        pair(far).wait_recv()
+        for i in range(2):
+            s = jnp.where(toward == i, 0, 1)
+            target = far * 2 + s
+            for yy in range(rings):
+                for xx, block_sum in enumerate(joined(far, s, yy)):
+                    k = i * freqs + yy * 2 + xx
+                    if relayed:
+                        fsend[target * freqs + yy * 2 + xx] = block_sum.astype(bf16)
+                        inward(target, k).start()
+                    else:
+                        pltpu.make_async_copy(rrecv.at[k], rrecv.at[k], r_recv.at[k]).wait()
+                        total = block_sum + rrecv[k].astype(f32)
+                        fsend[target * freqs + yy * 2 + xx] = total.astype(bf16)
+                        owner(target, xx, yy).start()
+
+    def ship_near():
+        pair(near).wait_recv()
+        s = 1 - z % 2
         for yy in range(rings):
-            re, im = [
-                pacc[h, part * rings + yy, core, :, lanes]
-                + precv[h, part * rings + yy, :, lanes].astype(f32)
-                for part in range(2)
-            ]
-            for xx in range(2):
-                cut = slice(xx * narrow, (xx + 1) * narrow)
-                joined = jnp.concatenate([re[:, cut], im[:, cut]], axis=1)
-                fsend[target * freqs + yy * 2 + xx] = joined.astype(bf16)
-
-                @pl.when(target == z)
-                def _():
-                    mine32[yy, xx] = joined
-
-        @pl.when(target == z)
-        def _():
-            for dx, dy in routes:
-                if dx or dy:
-                    neighbour(dx, dy).start()
-
-        @pl.when(target != z)
-        def _():
-            for dx, dy in routes:
-                owner(target, dx, dy).start()
+            for xx, block_sum in enumerate(joined(near, s, yy)):
+                target = near * 2 + s
+                fsend[target * freqs + yy * 2 + xx] = block_sum.astype(bf16)
+                owner(target, xx, yy).start()
+        for yy in range(rings):
+            for xx, block_sum in enumerate(joined(near, z % 2, yy)):
+                fsend[z * freqs + yy * 2 + xx] = block_sum.astype(bf16)
+                mine32[yy, xx] = block_sum
+        for dx, dy in routes:
+            if dx or dy:
+                neighbour(dx, dy).start()
 
     pl.semaphore_wait(ready, levels - 1)
-    far = 1 - z // 2
-    toward = jnp.where(z < levels // 2, 1, 0)
-    pair(far).wait_recv()
-    ship(far, toward)
-    ship(far, 1 - toward)
-    pair(1 - far).wait_recv()
-    ship(1 - far, 1 - z % 2)
-    ship(1 - far, z % 2)
+
+    @pl.when(at_end)
+    def _():
+        ship_far(True)
+        ship_near()
+
+    @pl.when(jnp.logical_not(at_end))
+    def _():
+        ship_near()
+        ship_far(False)
 
     out[me] = mine32[y, x]
     for dx, dy in reversed(routes):
@@ -490,8 +519,10 @@
             pltpu.make_async_copy(frecv.at[z, w], frecv.at[z, w], f_recv.at[w]).wait()
             out[w] = frecv[z, w].astype(f32)
 
-    for source in reversed(range(levels)):
-        @pl.when(source != z)
+    for source in range(levels):
+        outer_level = source in (0, levels - 1)
+
+        @pl.when((source != z) & (z == abs(source - 1) if outer_level else True))
         def _():
             pltpu.make_async_copy(frecv.at[source], frecv.at[source], q_recv.at[source]).wait()
             out[...] += frecv[source].astype(f32)
@@ -544,15 +575,16 @@
             pltpu.VMEM((pieces, 2, share_rows, width), bf16),
             pltpu.VMEM((pieces, 2, share_rows, width), bf16),
             pltpu.VMEM((pieces, 2, share_rows, width), bf16),
-            pltpu.VMEM((freqs, local, 2, rows, width), bf16),
-            pltpu.VMEM((freqs, SPLITS, 2, rows // SPLITS, width), bf16),
-            pltpu.VMEM((SPLITS, 2, share_rows, width), f32),
+            pltpu.VMEM((freqs, local, 2, rows, size // 2), bf16),
+            pltpu.VMEM((freqs, pieces // 2, 2, rows // SPLITS, width), bf16),
+            pltpu.VMEM((pieces // 2, 2, share_rows, width), f32),
             pltpu.VMEM((2, share_rows, width), f32),
             pltpu.VMEM((2, tiles, 2, rows, 2 * width), f32),
             pltpu.VMEM((2, tiles, rows, 2 * width), bf16),
             pltpu.VMEM((2, tiles, rows, 2 * width), bf16),
             pltpu.VMEM((levels * freqs, rows, width), bf16),
             pltpu.VMEM((levels, freqs, rows, width), bf16),
+            pltpu.VMEM((2 * freqs, rows, width), bf16),
             pltpu.VMEM((cols // 2, 2, rows, width), f32),
             dma, dma, dma((pieces,)),
             dma, dma((pieces,)),
@@ -560,7 +592,7 @@
             dma, dma((pieces,)),
             dma, dma, dma,
             dma, dma((2,)),
-            dma((levels,)), dma, dma((freqs,)),
+            dma((levels,)), dma((2 * freqs,)), dma, dma((freqs,)),
             pltpu.SemaphoreType.REGULAR,
         ],
         compiler_params=pltpu.CompilerParams(

time: 57.3 us -> 58.2 us (1.016)
  Pallas kernels: 54.9 us -> 56.2 us
    pallas_call x1, Pallas kernels: 54.9 us -> 56.2 us  [fused(): pl.pallas_call(functools.partial(kernel, sizes), out_shape=jax.ShapeDtype...]
where the time goes in v3:
time: 58.2 us; the launch traced here: 58 us
  Pallas kernels  56.2 us (97%)
  local copies, waits for them, and re-layouts  1.79 us (3%)
    pallas_call x1, Pallas kernels, fused(): pl.pallas_call(functools.partial(kernel, sizes), out_shape=jax.ShapeDtype...  56.2 us
    pallas_call x1, local copies, waits for them, and re-layouts, fused(): pl.pallas_call(functools.partial(kernel, sizes), out_shape=jax.ShapeDtype...  1.79 us

profile of v3, /device:TPU:0, one launch (start us, length us, event | category | flops | bytes accessed | tf_op | source)
XLA Modules:
  0.0 58.0 jit_solution(3276082785676326358)
XLA Ops:
  0.0 56.2 %prediction.1 = f32[4,128,128]{2,1,0:T(8,128)} custom-call(bf16[4,2,2,128,512]{4,3,2,1,0:T(8,128)(2,1)} %rec.1, f32[4,512]{1,0:T(4,128)} %vertical.1), custom_call_target="tpu_custom_call" | custom-call | tf_op jit(solution)/shard_map/prediction/pallas_call | solution.py:553
  56.2 1.8 %copy.4 = f32[4,128,128]{1,2,0:T(8,128)} copy(f32[4,128,128]{2,1,0:T(8,128)} %prediction.1) | data formatting | bytes 524288 | tf_op jit(solution)/shard_map/prediction/pallas_call | solution.py:553

commit v4 on v3

--- a/solution.py
+++ b/solution.py
@@ -9,8 +9,9 @@
 
 MESH = pl.DeviceIdType.MESH
 SPLITS = 4
-HOP = 3
-LEAD = 2
+HOP = 2
+AHEAD = 6
+SLACK = 2
 VMEM_MIB = 56
 
 
@@ -103,14 +104,13 @@
     v_sem, a_send, a_recv, s_send, s_recv, e_send, e_recv, x_send, x_recv, g_sem, g_send, g_recv, p_send, p_recv,
     q_recv, r_recv, f_send, f_recv, ready,
 ):
-    levels, freqs, cols, local, rows, size, width, splits = sizes
+    levels, freqs, cols, local, rows, size, width, splits, ahead = sizes
     depth, col = lax.axis_index("depth"), lax.axis_index("col")
     z, x = depth // 2, depth % 2
     y, core = col // 2, col % 2
     rings = cols // 2
     tiles = 2 * rings
     pieces = size // width * splits
-    ahead = pieces // 2
     plain = pieces - ahead
     sub = rows // splits
     share_rows = cols * sub // 2
@@ -162,29 +162,32 @@
     rt[...] = table[0 : own + 2 * local * freqs, :] * (1.0 / (2 * levels * local))
     local_last.wait()
 
-    @pl.loop(0, ahead)
-    def _(i):
-        r = i % splits
-        at = pl.ds(pl.multiple_of(r * sub, sub), sub)
-        part_lanes = pl.ds(aligned(i // splits, width), width)
-        last = pl.ds(pl.multiple_of(size // 2 + i // splits * width, width), width)
-        line = pl.ds(pl.multiple_of(col * rows + r * sub, sub), sub)
-        for w in range(freqs):
-            sum_re = sum_im = None
-            for l in range(local):
-                c = own + 2 * l * freqs + w
-                d = c + freqs
-                re = stage[w, l, 0, at, part_lanes].astype(f32)
-                im = stage[w, l, 1, at, part_lanes].astype(f32)
-                row_cos, row_sin = ct[line, c : c + 1], ct[line, d : d + 1]
-                col_cos, col_sin = rt[c : c + 1, last], rt[d : d + 1, last]
-                cosine = row_cos * col_cos - row_sin * col_sin
-                sine = row_sin * col_cos + row_cos * col_sin
-                plus_re, plus_im = re * cosine - im * sine, re * sine + im * cosine
-                sum_re = plus_re if sum_re is None else sum_re + plus_re
-                sum_im = plus_im if sum_im is None else sum_im + plus_im
-            presend[w, i, 0] = sum_re.astype(bf16)
-            presend[w, i, 1] = sum_im.astype(bf16)
+    @pl.when(z > 0)
+    def _():
+        @pl.loop(0, ahead)
+        def _(i):
+            r = (plain + i) % splits
+            j = (plain + i) // splits
+            at = pl.ds(pl.multiple_of(r * sub, sub), sub)
+            part_lanes = pl.ds(pl.multiple_of(j * width - size // 2, width), width)
+            last = pl.ds(aligned(j, width), width)
+            line = pl.ds(pl.multiple_of(col * rows + r * sub, sub), sub)
+            for w in range(freqs):
+                sum_re = sum_im = None
+                for l in range(local):
+                    c = own + 2 * l * freqs + w
+                    d = c + freqs
+                    re = stage[w, l, 0, at, part_lanes].astype(f32)
+                    im = stage[w, l, 1, at, part_lanes].astype(f32)
+                    row_cos, row_sin = ct[line, c : c + 1], ct[line, d : d + 1]
+                    col_cos, col_sin = rt[c : c + 1, last], rt[d : d + 1, last]
+                    cosine = row_cos * col_cos - row_sin * col_sin
+                    sine = row_sin * col_cos + row_cos * col_sin
+                    plus_re, plus_im = re * cosine - im * sine, re * sine + im * cosine
+                    sum_re = plus_re if sum_re is None else sum_re + plus_re
+                    sum_im = plus_im if sum_im is None else sum_im + plus_im
+                presend[w, i, 0] = sum_re.astype(bf16)
+                presend[w, i, 1] = sum_im.astype(bf16)
 
     pl.semaphore_wait(barrier, greeted)
 
@@ -212,12 +215,15 @@
         return remote(src, dst, g_send, g_recv, device(z, xx, yy, x))
 
     routes = [(dx, dy) for dy in reversed(range(rings)) for dx in (1, 0)]
-    for dx, dy in routes:
-        if dx or dy:
-            early(dx, dy).start()
-        else:
-            pl.when(core == x)(lambda: early(dx, dy, near=True).start())
-            pl.when(core != x)(lambda: early(dx, dy).start())
+    @pl.when(z > 0)
+    def _():
+        for dx, dy in routes:
+            if dx or dy:
+                early(dx, dy).start()
+            else:
+                pl.when(core == x)(lambda: early(dx, dy, near=True).start())
+                pl.when(core != x)(lambda: early(dx, dy).start())
+
     for n in range(pieces):
         for dx, dy in routes:
             if dx or dy:
@@ -282,13 +288,13 @@
                 sum_re = plus_re if sum_re is None else sum_re + plus_re
                 sum_im = plus_im if sum_im is None else sum_im + plus_im
 
-            @pl.when(n < plain)
+            @pl.when((n < plain) | (z == 0))
             def _():
                 packed = pl.ds(aligned(t, sub), sub)
                 sbuf[n, 0, packed, :] = sum_re.astype(bf16)
                 sbuf[n, 1, packed, :] = sum_im.astype(bf16)
 
-        pl.when(n < plain)(lambda: share(n).start())
+        pl.when((n < plain) | (z == 0))(lambda: share(n).start())
 
     def put_tail(n, half, deeper_at):
         j, first, lanes = place(n)
@@ -379,28 +385,35 @@
         result = jnp.dot(tl[:, begin:end], prod[begin:end, lanes], preferred_element_type=f32)
         return result.reshape(tiles, 2, rows, block)
 
-    pltpu.make_async_copy(
-        sbuf.at[pl.ds(plain, ahead)], sbuf.at[pl.ds(plain, ahead)], g_recv
-    ).wait()
-    for i in range(ahead):
-        share(plain + i).start()
-    above, soon = HOP * (levels - 1 - z), LEAD * (levels - 1 - z)
-
-    @pl.loop(0, max(pieces, plain + 2 + HOP * (levels - 1)))
+    @pl.when(z > 0)
+    def _():
+        whole = sbuf.at[pl.ds(plain, ahead)]
+        pltpu.make_async_copy(whole, whole, g_recv).wait()
+        for i in range(ahead):
+            share(plain + i).start()
+
+    above = HOP * (levels - 1 - z) + jnp.where(z == 0, SLACK, 0)
+    soon = jnp.where(z == 0, plain + 1, HOP * (levels - 1 - z))
+    after = jnp.where(z == 0, 2, 0)
+    ripe = jnp.where(z == 0, max(pieces - 1, HOP * (levels - 1) + SLACK + pieces // 2 + 1), pieces - 1)
+
+    @pl.loop(0, max(pieces + 2, plain + 2 + SLACK + HOP * (levels - 1)))
     def _(s):
         pl.when(s < pieces)(lambda: phase(s))
-        c = s - above - 1
-        pl.when((c >= 0) & (c < plain))(lambda: chain(c))
         e = s - soon
         pl.when((e >= 0) & (e < ahead))(lambda: chain(plain + e, True))
+        g = s - after
+        pl.when((g >= plain) & (g < pieces))(lambda: held(g))
+        c = s - above - 1
         f = c - 1
         pl.when((f >= 0) & (f < plain))(lambda: finish(f))
-        pl.when((s >= plain) & (s < pieces))(lambda: held(s))
-
-        @pl.when(s == pieces - 1)
+
+        @pl.when(s == ripe)
         def _():
-            middle(1)
-            pacc[1] = outer(1, span, 2 * span)
+            middle(0)
+            pacc[0] = outer(0, 0, span)
+
+        pl.when((c >= 0) & (c < plain))(lambda: chain(c))
 
     def pair(h):
         return remote(psend.at[h], precv.at[h], p_send, p_recv.at[h], other_core)
@@ -413,14 +426,14 @@
         pair(h).start()
 
     def low_block():
-        pacc[0] = outer(0, 0, 2 * span)
+        pacc[0] += outer(0, span, 2 * span)
         swap(0)
 
     def high_block():
-        pacc[1] += outer(1, 0, span)
+        pacc[1] = outer(1, 0, 2 * span)
         swap(1)
 
-    middle(0)
+    middle(1)
 
     @pl.when(z % 2 == 0)
     def _():
@@ -535,8 +548,8 @@
     sent(sbuf.at[:, :, pl.ds(0, share_rows), :], s_send)
     pl.when(z > 0)(lambda: sent(eout, e_send))
     sent(xsend, x_send)
-    pl.when(core == x)(lambda: sent(presend.at[pl.ds(0, freqs - 1)], g_send))
-    pl.when(core != x)(lambda: sent(presend, g_send))
+    pl.when((z > 0) & (core == x))(lambda: sent(presend.at[pl.ds(0, freqs - 1)], g_send))
+    pl.when((z > 0) & (core != x))(lambda: sent(presend, g_send))
     sent(psend, p_send)
     sent(fsend.at[pl.ds(0, levels * freqs - 1)], f_send)
 
@@ -547,7 +560,7 @@
     levels, width = depths // 2, 2 * size // depths
     tiles = cols
     pieces, share_rows = size // width * SPLITS, rows * cols // SPLITS // 2
-    sizes = (levels, freqs, cols, local, rows, size, width, SPLITS)
+    sizes = (levels, freqs, cols, local, rows, size, width, SPLITS, AHEAD)
     f32, bf16 = jnp.float32, jnp.bfloat16
     dma = pltpu.SemaphoreType.DMA
     packed = pl.pallas_call(
@@ -576,8 +589,8 @@
             pltpu.VMEM((pieces, 2, share_rows, width), bf16),
             pltpu.VMEM((pieces, 2, share_rows, width), bf16),
             pltpu.VMEM((freqs, local, 2, rows, size // 2), bf16),
-            pltpu.VMEM((freqs, pieces // 2, 2, rows // SPLITS, width), bf16),
-            pltpu.VMEM((pieces // 2, 2, share_rows, width), f32),
+            pltpu.VMEM((freqs, AHEAD, 2, rows // SPLITS, width), bf16),
+            pltpu.VMEM((AHEAD, 2, share_rows, width), f32),
             pltpu.VMEM((2, share_rows, width), f32),
             pltpu.VMEM((2, tiles, 2, rows, 2 * width), f32),
             pltpu.VMEM((2, tiles, rows, 2 * width), bf16),

time: 58.2 us -> 57.4 us (0.986)
  Pallas kernels: 56.2 us -> 55.4 us
    pallas_call x1, Pallas kernels: 56.2 us -> 55.4 us  [fused(): pl.pallas_call(functools.partial(kernel, sizes), out_shape=jax.ShapeDtype...]
where the time goes in v4:
time: 57.4 us; the launch traced here: 57.2 us
  Pallas kernels  55.4 us (97%)
  local copies, waits for them, and re-layouts  1.79 us (3%)
    pallas_call x1, Pallas kernels, fused(): pl.pallas_call(functools.partial(kernel, sizes), out_shape=jax.ShapeDtype...  55.4 us
    pallas_call x1, local copies, waits for them, and re-layouts, fused(): pl.pallas_call(functools.partial(kernel, sizes), out_shape=jax.ShapeDtype...  1.79 us

profile of v4, /device:TPU:0, one launch (start us, length us, event | category | flops | bytes accessed | tf_op | source)
XLA Modules:
  0.0 57.2 jit_solution(10707421846398448789)
XLA Ops:
  0.0 55.4 %prediction.1 = f32[4,128,128]{2,1,0:T(8,128)} custom-call(bf16[4,2,2,128,512]{4,3,2,1,0:T(8,128)(2,1)} %rec.1, f32[4,512]{1,0:T(4,128)} %vertical.1), custom_call_target="tpu_custom_call" | custom-call | tf_op jit(solution)/shard_map/prediction/pallas_call | solution.py:566
  55.4 1.8 %copy.4 = f32[4,128,128]{1,2,0:T(8,128)} copy(f32[4,128,128]{2,1,0:T(8,128)} %prediction.1) | data formatting | bytes 524288 | tf_op jit(solution)/shard_map/prediction/pallas_call | solution.py:566

commit v5 on v4

--- a/solution.py
+++ b/solution.py
@@ -11,7 +11,7 @@
 SPLITS = 4
 HOP = 2
 AHEAD = 6
-SLACK = 2
+SLACK = 3
 VMEM_MIB = 56
 
 
@@ -311,8 +311,9 @@
                 base = (j // 2 * local + l) * 2 * block + j % 2 * width
                 fore = pl.ds(pl.multiple_of(base, width), width)
                 back = pl.ds(pl.multiple_of(base + block, width), width)
-                ts[l, at, lanes] = re.astype(bf16)
-                ts[l, low, lanes] = im.astype(bf16)
+                inside = pl.ds(aligned(j % 2, width), width)
+                ts[l, j // 2, at, inside] = re.astype(bf16)
+                ts[l, j // 2, low, inside] = im.astype(bf16)
                 tl[at, fore] = re.astype(bf16)
                 tl[low, back] = re.astype(bf16)
                 tl[at, back] = (-im).astype(bf16)
@@ -370,20 +371,13 @@
         put_tail(n, core, lambda at: [keep[n - plain, part, at, :] for part in range(2)])
         finish(n)
 
-    span = local * 2 * block
-
     def middle(h):
-        lanes = slice(h * block, (h + 1) * block)
-        for l in range(local):
-            result = jnp.dot(ml[l], ts[l, :, lanes], preferred_element_type=f32).astype(bf16)
+        @pl.loop(0, local)
+        def _(l):
+            result = jnp.dot(ml[l], ts[l, h], preferred_element_type=f32).astype(bf16)
             for half in range(2):
-                base = half * span + l * 2 * block
-                prod[base : base + 2 * block, lanes] = result[half * 2 * block : (half + 1) * 2 * block]
-
-    def outer(h, begin, end):
-        lanes = slice(h * block, (h + 1) * block)
-        result = jnp.dot(tl[:, begin:end], prod[begin:end, lanes], preferred_element_type=f32)
-        return result.reshape(tiles, 2, rows, block)
+                into = pl.ds(aligned(half * local + l, 2 * block), 2 * block)
+                prod[h, into, :] = result[half * 2 * block : (half + 1) * 2 * block]
 
     @pl.when(z > 0)
     def _():
@@ -395,25 +389,26 @@
     above = HOP * (levels - 1 - z) + jnp.where(z == 0, SLACK, 0)
     soon = jnp.where(z == 0, plain + 1, HOP * (levels - 1 - z))
     after = jnp.where(z == 0, 2, 0)
-    ripe = jnp.where(z == 0, max(pieces - 1, HOP * (levels - 1) + SLACK + pieces // 2 + 1), pieces - 1)
-
-    @pl.loop(0, max(pieces + 2, plain + 2 + SLACK + HOP * (levels - 1)))
+    ripe = max(pieces - 1, HOP * (levels - 1) + SLACK + pieces // 2 + 1)
+    steps = max(pieces + 2, plain + 2 + SLACK + HOP * (levels - 1))
+
+    @pl.loop(0, steps + 2)
     def _(s):
+        c = s - above - 1
+        f = c - 1
+        due = (c >= 0) & (c < plain)
+        pl.when(due & ((z == 1) | (z == 2)))(lambda: chain(c))
         pl.when(s < pieces)(lambda: phase(s))
         e = s - soon
         pl.when((e >= 0) & (e < ahead))(lambda: chain(plain + e, True))
         g = s - after
         pl.when((g >= plain) & (g < pieces))(lambda: held(g))
-        c = s - above - 1
-        f = c - 1
+        pl.when(due & ((z == levels - 1) | (z == 0)))(lambda: chain(c))
         pl.when((f >= 0) & (f < plain))(lambda: finish(f))
 
-        @pl.when(s == ripe)
-        def _():
-            middle(0)
-            pacc[0] = outer(0, 0, span)
-
-        pl.when((c >= 0) & (c < plain))(lambda: chain(c))
+        begin = jnp.where(z == 0, ripe, steps)
+        then = jnp.where(z == 0, steps, steps + 1)
+        pl.when((s == begin) | (s == then))(lambda: middle(jnp.where(s == begin, 0, 1)))
 
     def pair(h):
         return remote(psend.at[h], precv.at[h], p_send, p_recv.at[h], other_core)
@@ -425,25 +420,14 @@
 
         pair(h).start()
 
-    def low_block():
-        pacc[0] += outer(0, span, 2 * span)
-        swap(0)
-
-    def high_block():
-        pacc[1] = outer(1, 0, 2 * span)
-        swap(1)
-
-    middle(1)
-
-    @pl.when(z % 2 == 0)
-    def _():
-        high_block()
-        low_block()
-
-    @pl.when(z % 2 == 1)
-    def _():
-        low_block()
-        high_block()
+    lead = jnp.where(z % 2 == 0, 1, 0)
+
+    @pl.loop(0, 2)
+    def _(i):
+        h = jnp.where(i == 0, lead, 1 - lead)
+        result = jnp.dot(tl[...], prod[h], preferred_element_type=f32)
+        pacc[h] = result.reshape(tiles, 2, rows, block)
+        swap(h)
 
     narrow = width // 2
     near, far = z // 2, 1 - z // 2
@@ -579,8 +563,8 @@
             pltpu.VMEM((local, 2, cols, rows, size), bf16),
             pltpu.VMEM((local, 2 * size, 2 * size), bf16),
             pltpu.VMEM((2 * size, local * 2 * size), bf16),
-            pltpu.VMEM((local, 2 * size, size), bf16),
-            pltpu.VMEM((local * 2 * size, size), bf16),
+            pltpu.VMEM((local, 2, 2 * size, 2 * width), bf16),
+            pltpu.VMEM((2, local * 2 * size, 2 * width), bf16),
             pltpu.VMEM((local - 1, 2, size, size), f32),
             pltpu.VMEM((pieces, 2, 2 * share_rows, width), bf16),
             pltpu.VMEM((pieces, 2, share_rows, width), bf16),

time: 57.4 us -> 56.1 us (0.977)
  Pallas kernels: 55.4 us -> 54.2 us
    pallas_call x1, Pallas kernels: 55.4 us -> 54.2 us  [fused(): pl.pallas_call(functools.partial(kernel, sizes), out_shape=jax.ShapeDtype...]
where the time goes in v5:
time: 56.1 us; the launch traced here: 56 us
  Pallas kernels  54.2 us (97%)
  local copies, waits for them, and re-layouts  1.79 us (3%)
    pallas_call x1, Pallas kernels, fused(): pl.pallas_call(functools.partial(kernel, sizes), out_shape=jax.ShapeDtype...  54.2 us
    pallas_call x1, local copies, waits for them, and re-layouts, fused(): pl.pallas_call(functools.partial(kernel, sizes), out_shape=jax.ShapeDtype...  1.79 us

profile of v5, /device:TPU:0, one launch (start us, length us, event | category | flops | bytes accessed | tf_op | source)
XLA Modules:
  0.0 56.0 jit_solution(2683581257979029529)
XLA Ops:
  0.0 54.2 %prediction.1 = f32[4,128,128]{2,1,0:T(8,128)} custom-call(bf16[4,2,2,128,512]{4,3,2,1,0:T(8,128)(2,1)} %rec.1, f32[4,512]{1,0:T(4,128)} %vertical.1), custom_call_target="tpu_custom_call" | custom-call | tf_op jit(solution)/shard_map/prediction/pallas_call | solution.py:550
  54.2 1.8 %copy.4 = f32[4,128,128]{1,2,0:T(8,128)} copy(f32[4,128,128]{2,1,0:T(8,128)} %prediction.1) | data formatting | bytes 524288 | tf_op jit(solution)/shard_map/prediction/pallas_call | solution.py:550

commit v6 on v5

--- a/solution.py
+++ b/solution.py
@@ -10,9 +10,9 @@
 MESH = pl.DeviceIdType.MESH
 SPLITS = 4
 HOP = 2
-AHEAD = 6
-SLACK = 3
-VMEM_MIB = 56
+AHEAD = 7
+SLACK = 2
+VMEM_MIB = 53
 
 
 def prefix(x, axis, combine, identity):

time: 56.1 us -> 54.8 us (0.977)
  Pallas kernels: 54.2 us -> 53.1 us
    pallas_call x1, Pallas kernels: 54.2 us -> 53.1 us  [fused(): pl.pallas_call(functools.partial(kernel, sizes), out_shape=jax.ShapeDtype...]
    pallas_call x1, local copies, waits for them, and re-layouts: 1.79 us -> 0.84 us  [fused(): pl.pallas_call(functools.partial(kernel, sizes), out_shape=jax.ShapeDtype...]
    unnamed x0 -> x2, local copies, waits for them, and re-layouts: none -> 0.7 us
where the time goes in v6:
time: 54.8 us; the launch traced here: 54.6 us
  Pallas kernels  53.1 us (97%)
  local copies, waits for them, and re-layouts  1.53 us (3%)
    pallas_call x1, Pallas kernels, fused(): pl.pallas_call(functools.partial(kernel, sizes), out_shape=jax.ShapeDtype...  53.1 us

profile of v6, /device:TPU:0, one launch (start us, length us, event | category | flops | bytes accessed | tf_op | source)
XLA Modules:
  0.0 54.6 jit_solution(8930908049927255066)
XLA Ops:
  0.0 0.0 copy-start
  0.0 0.7 %copy-done = f32[4,512]{1,0:T(4,128)S(1)} copy-done((f32[4,512]{1,0:T(4,128)S(1)}, f32[4,512]{1,0:T(4,128)}, u32[]{:S(2)}) %copy-start) | copy-done | bytes 8216
  0.7 53.1 %prediction.1 = f32[4,128,128]{2,1,0:T(8,128)S(1)} custom-call(bf16[4,2,2,128,512]{4,3,2,1,0:T(8,128)(2,1)} %rec.1, f32[4,512]{1,0:T(4,128)S(1)} %copy-done), custom_call_target="tpu_custom_call" | custom-call | tf_op jit(solution)/shard_map/prediction/pallas_call | solution.py:550
  53.8 0.8 %copy.4 = f32[4,128,128]{1,2,0:T(8,128)} copy(f32[4,128,128]{2,1,0:T(8,128)S(1)} %prediction.1) | data formatting | bytes 524288 | tf_op jit(solution)/shard_map/prediction/pallas_call | solution.py:550
Async XLA Ops:
  0.0 0.7 %copy-start = (f32[4,512]{1,0:T(4,128)S(1)}, f32[4,512]{1,0:T(4,128)}, u32[]{:S(2)}) copy-start(f32[4,512]{1,0:T(4,128)} %vertical.1) | copy-start | bytes 24580

commit v7 on v6

--- a/solution.py
+++ b/solution.py
@@ -596,7 +596,7 @@
             collective_id=0, has_side_effects=True, vmem_limit_bytes=VMEM_MIB * 1024 * 1024
         ),
         name="prediction",
-    )(recorded, vertical)
+    )(recorded, pltpu.with_memory_space_constraint(vertical, pltpu.HBM))
     return packed.reshape(freqs, rows, 2, width // 2).transpose(0, 2, 1, 3)
 
 

time: 54.8 us -> 54.1 us (0.987)
  local copies, waits for them, and re-layouts: 1.53 us -> 0.84 us
    unnamed x2 -> x0, local copies, waits for them, and re-layouts: 0.7 us -> none
where the time goes in v7:
time: 54.1 us; the launch traced here: 53.9 us
  Pallas kernels  53.1 us (98%)
  local copies, waits for them, and re-layouts  0.84 us (2%)
    pallas_call x1, Pallas kernels, fused(): pl.pallas_call(functools.partial(kernel, sizes), out_shape=jax.ShapeDtype...  53.1 us

profile of v7, /device:TPU:0, one launch (start us, length us, event | category | flops | bytes accessed | tf_op | source)
XLA Modules:
  0.0 53.9 jit_solution(16118895223110583011)
XLA Ops:
  0.0 53.1 %prediction.1 = f32[4,128,128]{2,1,0:T(8,128)S(1)} custom-call(bf16[4,2,2,128,512]{4,3,2,1,0:T(8,128)(2,1)} %rec.1, f32[4,512]{1,0:T(4,128)} %vertical.1), custom_call_target="tpu_custom_call" | custom-call | tf_op jit(solution)/shard_map/prediction/pallas_call | solution.py:550
  53.1 0.8 %copy.4 = f32[4,128,128]{1,2,0:T(8,128)} copy(f32[4,128,128]{2,1,0:T(8,128)S(1)} %prediction.1) | data formatting | bytes 524288 | tf_op jit(solution)/shard_map/prediction/pallas_call | solution.py:550
